TPU v7x, 128 devices: a whole 4x4x4 slice. The times are simulated.
128 devices in a mesh: row: 8 (over y, z_lo), col: 16 (over z_hi, x, core).
Axes of the slice: x: 4, y: 4, z: 4 (z_hi: 2, z_lo: 2; z = z_hi * 2 + z_lo), core: 2. Of those that a mesh axis runs over, the one named last changes fastest.
Arguments:
- homolog_stack: bfloat16 [512, 512, 256], P(('row', 'col')), may hold values from -6 to 6
- per_amino_features: bfloat16 [512, 256], P(('row', 'col')), may hold values from -6 to 6
- asking_matrix: bfloat16 [256, 256], replicated, may hold values from -24 to 24
- lookup_matrix: bfloat16 [256, 256], replicated, may hold values from -0.375 to 0.375
- content_matrix: bfloat16 [256, 256], replicated, may hold values from -0.375 to 0.375
- sigmoid_scaling_matrix: bfloat16 [256, 256], replicated, may hold values from -0.375 to 0.375
- attention_result_matrix: bfloat16 [256, 256], replicated, may hold values from -0.375 to 0.375
- stack_transition_expand_matrix: bfloat16 [256, 1024], replicated, may hold values from -0.375 to 0.375
- stack_transition_shrink_matrix: bfloat16 [1024, 256], replicated, may hold values from -0.1875 to 0.1875
- former_factor_matrix: bfloat16 [256, 32], replicated, may hold values from -0.375 to 0.375
- latter_factor_matrix: bfloat16 [256, 32], replicated, may hold values from -0.375 to 0.375
- factor_mean_projection: bfloat16 [1024, 128], replicated, may hold values from -1.1953125 to 1.1953125
- row_amino_embedding: bfloat16 [256, 128], replicated, may hold values from -0.375 to 0.375
- column_amino_embedding: bfloat16 [256, 128], replicated, may hold values from -0.375 to 0.375
- offset_embedding_matrix: bfloat16 [65, 128], replicated, may hold values from -3 to 3
- grid_transition_expand: bfloat16 [128, 512], replicated, may hold values from -0.5 to 0.5
- grid_transition_shrink: bfloat16 [512, 128], replicated, may hold values from -0.25 to 0.25
- distance_bins_matrix: bfloat16 [128, 64], replicated, may hold values from -0.5 to 0.5
Outputs:
- alignment_output: bfloat16 [512, 512, 256], P(None, ('row', 'col'))
- pair_output: bfloat16 [512, 512, 128], P('row', 'col')
- distogram: bfloat16 [512, 512, 64], P('row', 'col')
All inputs are finite; a program needn't handle non-finite values.
Results may differ from a plain program's by a relative error of at most 0.011.
The roundings to bfloat16 on the way count: a program that leaves them out, or rounds other values in their place, can miss the bound.
Values may be sent and summed in bfloat16 or wider, within the bound.
A program may use at most 256 MiB of HBM per device.

v0:
```python
import math

import jax
import jax.numpy as jnp
from jax import lax
from jax.sharding import PartitionSpec as P

HEADS = 8
HEAD = 32
CLIP = 32


def spread_2(block, axis, source):
    block = jnp.where(lax.axis_index(axis) == source, block, jnp.zeros_like(block))
    return lax.psum(block, axis)


def standardize_features(values):
    middle = jnp.mean(values, -1, keepdims=True)
    centred = values - middle
    spread = jnp.mean(centred * centred, -1, keepdims=True)
    return centred * lax.rsqrt(spread + 1e-05)


def alignment_layer(
    block_piece,
    asking_matrix,
    lookup_matrix,
    content_matrix,
    sigmoid_scaling_matrix,
    attention_result_matrix,
    stack_transition_expand_matrix,
    stack_transition_shrink_matrix,
):
    count_seq, count_res, feature_width = block_piece.shape
    start = block_piece.astype(jnp.float32).reshape(-1, feature_width)
    standardized = standardize_features(start).astype(jnp.bfloat16)
    query = jnp.dot(standardized, asking_matrix, preferred_element_type=jnp.float32).astype(
        jnp.bfloat16
    )
    key_rows = jnp.dot(standardized, lookup_matrix, preferred_element_type=jnp.float32).astype(
        jnp.bfloat16
    )
    value_rows = jnp.dot(standardized, content_matrix, preferred_element_type=jnp.float32).astype(
        jnp.bfloat16
    )
    gate = jax.nn.sigmoid(
        jnp.dot(standardized, sigmoid_scaling_matrix, preferred_element_type=jnp.float32)
    )
    query = query.reshape(count_seq, count_res, HEADS, HEAD)
    key_rows = key_rows.reshape(count_seq, count_res, HEADS, HEAD)
    value_rows = value_rows.reshape(count_seq, count_res, HEADS, HEAD)
    scores = jnp.einsum(
        "sihd,tihd->ihst", query, key_rows, preferred_element_type=jnp.float32
    ) / math.sqrt(HEAD)
    weights = jax.nn.softmax(scores, -1).astype(jnp.bfloat16)
    attended = jnp.einsum(
        "ihst,tihd->sihd", weights, value_rows, preferred_element_type=jnp.float32
    ).reshape(-1, feature_width)
    mixed = (attended * gate).astype(jnp.bfloat16)
    first_part = start + jnp.dot(mixed, attention_result_matrix, preferred_element_type=jnp.float32)
    hidden_units = jax.nn.relu(
        jnp.dot(
            standardize_features(first_part).astype(jnp.bfloat16),
            stack_transition_expand_matrix,
            preferred_element_type=jnp.float32,
        )
    ).astype(jnp.bfloat16)
    second_part = first_part + jnp.dot(
        hidden_units, stack_transition_shrink_matrix, preferred_element_type=jnp.float32
    )
    return second_part.reshape(count_seq, count_res, feature_width)


def pair_block(
    a_u,
    b_v,
    left_u,
    right_v,
    start_u,
    start_v,
    offset_embedding_matrix,
    factor_mean_projection,
    grid_transition_expand,
    grid_transition_shrink,
    distance_bins_matrix,
):
    count_seq, count_u, factor = a_u.shape
    count_v = b_v.shape[1]
    feature_width = left_u.shape[1]
    step_rows = max(1, min(count_u, 1024 // count_v))
    tile_collection = count_u // step_rows
    a_blocks = a_u.reshape(count_seq, tile_collection, step_rows, factor).transpose(1, 0, 2, 3)
    left_blocks = left_u.reshape(tile_collection, step_rows, feature_width)
    flat_v = b_v.reshape(count_seq, count_v * factor)
    columns = start_v + jnp.arange(count_v, dtype=jnp.int32)
    bins = jnp.arange(2 * CLIP + 1, dtype=jnp.int32)

    def one_block(inputs):
        a_blk, left_blk, index = inputs
        outer = lax.dot_general(
            a_blk.reshape(count_seq, step_rows * factor),
            flat_v,
            (((0,), (0,)), ((), ())),
            preferred_element_type=jnp.float32,
        )
        outer = (
            outer.reshape(step_rows, factor, count_v, factor)
            .transpose(0, 2, 1, 3)
            .reshape(step_rows * count_v, factor * factor)
        )
        outer = (outer / count_seq).astype(jnp.bfloat16)
        projected = jnp.dot(outer, factor_mean_projection, preferred_element_type=jnp.float32)
        rows_here = start_u + index * step_rows + jnp.arange(step_rows, dtype=jnp.int32)
        offset = jnp.clip(columns[None, :] - rows_here[:, None], -CLIP, CLIP) + CLIP
        onehot = (offset[:, :, None] == bins).astype(jnp.bfloat16).reshape(-1, 2 * CLIP + 1)
        relative = jnp.dot(onehot, offset_embedding_matrix, preferred_element_type=jnp.float32)
        embedded = (
            left_blk.astype(jnp.float32)[:, None, :] + right_v.astype(jnp.float32)[None, :, :]
        ).reshape(-1, feature_width)
        start_pair = embedded + relative + projected
        hidden_units = jax.nn.relu(
            jnp.dot(
                standardize_features(start_pair).astype(jnp.bfloat16),
                grid_transition_expand,
                preferred_element_type=jnp.float32,
            )
        ).astype(jnp.bfloat16)
        final = start_pair + jnp.dot(
            hidden_units, grid_transition_shrink, preferred_element_type=jnp.float32
        )
        rounded = final.astype(jnp.bfloat16)
        logits = jnp.dot(rounded, distance_bins_matrix, preferred_element_type=jnp.float32)
        return (
            rounded.reshape(step_rows, count_v, feature_width),
            logits.reshape(step_rows, count_v, -1),
        )

    pairs, logits = lax.map(
        one_block, (a_blocks, left_blocks, jnp.arange(tile_collection, dtype=jnp.int32))
    )
    return (pairs.reshape(count_u, count_v, feature_width), logits.reshape(count_u, count_v, -1))


def shards(
    homolog_stack,
    per_amino_features,
    asking_matrix,
    lookup_matrix,
    content_matrix,
    sigmoid_scaling_matrix,
    attention_result_matrix,
    stack_transition_expand_matrix,
    stack_transition_shrink_matrix,
    former_factor_matrix,
    latter_factor_matrix,
    factor_mean_projection,
    row_amino_embedding,
    column_amino_embedding,
    offset_embedding_matrix,
    grid_transition_expand,
    grid_transition_shrink,
    distance_bins_matrix,
):
    row_count = lax.axis_size("row")
    col_count = lax.axis_size("col")
    whole_mesh_axes = row_count * col_count
    homolog_shard_here, amino_collection, feature_width = homolog_stack.shape
    amino_shard_here = amino_collection // whole_mesh_axes
    fragment_collection = homolog_stack.reshape(
        1, homolog_shard_here, whole_mesh_axes, amino_shard_here, feature_width
    )
    moved = lax.all_to_all(
        fragment_collection, ("row", "col"), split_axis=2, concat_axis=0, tiled=True
    )
    local_part = moved.reshape(-1, amino_shard_here, feature_width)
    count_seq = local_part.shape[0]
    refreshed_stack = alignment_layer(
        local_part,
        asking_matrix,
        lookup_matrix,
        content_matrix,
        sigmoid_scaling_matrix,
        attention_result_matrix,
        stack_transition_expand_matrix,
        stack_transition_shrink_matrix,
    )
    alignment_output = refreshed_stack.astype(jnp.bfloat16)
    standardized = (
        standardize_features(refreshed_stack).astype(jnp.bfloat16).reshape(-1, feature_width)
    )
    left_opm = (
        jnp.dot(standardized, former_factor_matrix, preferred_element_type=jnp.float32)
        .astype(jnp.bfloat16)
        .reshape(count_seq, amino_shard_here, -1)
    )
    right_opm = (
        jnp.dot(standardized, latter_factor_matrix, preferred_element_type=jnp.float32)
        .astype(jnp.bfloat16)
        .reshape(count_seq, amino_shard_here, -1)
    )
    left_pair = jnp.dot(
        per_amino_features, row_amino_embedding, preferred_element_type=jnp.float32
    ).astype(jnp.bfloat16)
    right_pair = jnp.dot(
        per_amino_features, column_amino_embedding, preferred_element_type=jnp.float32
    ).astype(jnp.bfloat16)
    row_len = amino_collection // row_count
    col_len = amino_collection // col_count
    ratio = col_count // row_count
    row_a, row_b, row_left, row_right = (
        lax.all_gather(left_opm, "col", axis=1, tiled=True),
        lax.all_gather(right_opm, "col", axis=1, tiled=True),
        lax.all_gather(left_pair, "col", axis=0, tiled=True),
        lax.all_gather(right_pair, "col", axis=0, tiled=True),
    )
    offset = lax.axis_index("col") % ratio * col_len
    part_a = lax.dynamic_slice_in_dim(row_a, offset, col_len, 1)
    part_b = lax.dynamic_slice_in_dim(row_b, offset, col_len, 1)
    part_left = lax.dynamic_slice_in_dim(row_left, offset, col_len, 0)
    part_right = lax.dynamic_slice_in_dim(row_right, offset, col_len, 0)
    col_a, col_b, col_left, col_right = (
        spread_2(part_a, "row", lax.axis_index("col") // ratio),
        spread_2(part_b, "row", lax.axis_index("col") // ratio),
        spread_2(part_left, "row", lax.axis_index("col") // ratio),
        spread_2(part_right, "row", lax.axis_index("col") // ratio),
    )
    row_start = lax.axis_index("row") * row_len
    col_start = lax.axis_index("col") * col_len
    pair_output, logits = pair_block(
        row_a,
        col_b,
        row_left,
        col_right,
        row_start,
        col_start,
        offset_embedding_matrix,
        factor_mean_projection,
        grid_transition_expand,
        grid_transition_shrink,
        distance_bins_matrix,
    )
    ignored, mirror = pair_block(
        col_a,
        row_b,
        col_left,
        row_right,
        col_start,
        row_start,
        offset_embedding_matrix,
        factor_mean_projection,
        grid_transition_expand,
        grid_transition_shrink,
        distance_bins_matrix,
    )
    distogram = (logits + mirror.transpose(1, 0, 2)).astype(jnp.bfloat16)
    return (alignment_output, pair_output, distogram)


def solution(mesh):
    placed = (
        P(("row", "col"), None, None),
        P(("row", "col"), None),
        P(),
        P(),
        P(),
        P(),
        P(),
        P(),
        P(),
        P(),
        P(),
        P(),
        P(),
        P(),
        P(),
        P(),
        P(),
        P(),
    )
    return jax.shard_map(
        shards,
        mesh=mesh,
        in_specs=placed,
        out_specs=(P(None, ("row", "col"), None), P("row", "col", None), P("row", "col", None)),
        check_vma=False,
    )
```

profile of v0, /device:TPU:7, one launch (start us, length us, event | category | flops | bytes accessed | tf_op | source)
XLA Modules:
  0.0 482.0 jit_solution(15032839137248058428)
XLA Ops:
  7.2 2.1 copy.89
  9.7 28.2 %all_to_all.4 = bf16[1,4,128,4,256]{4,3,1,0,2:T(4,128)(2,1)S(1)} all-to-all(bf16[1,4,128,4,256]{4,3,1,0,2:T(4,128)(2,1)S(1)} %copy.90), channel_id=1, replica_groups=mesh['row'=8,'col'=16] {'row','col'}, dimensions={2} | all-to-all | bytes 2097152 | tf_op jit(solution)/shard_map/all_to_all | solution.py:173
  39.1 1.4 multiply_reduce_fusion.5
  40.9 2.0 convert_bitcast_fusion
  42.9 2.0 reshape.309
  44.9 1.7 convolution_convert_fusion.1
  46.6 5.8 %reshape.293 = bf16[512,4,8,32]{3,2,1,0:T(8,128)(2,1)} reshape(bf16[2048,256]{1,0:T(8,128)(2,1)} %convolution_convert_fusion.1) | data formatting | bytes 2097152 | tf_op jit(solution)/shard_map/reshape | solution.py:50
  52.4 1.7 convolution_convert_fusion
  54.2 6.2 %reshape.294 = bf16[512,4,8,32]{3,2,1,0:T(8,128)(2,1)} reshape(bf16[2048,256]{1,0:T(8,128)(2,1)} %convolution_convert_fusion) | data formatting | bytes 2097152 | tf_op jit(solution)/shard_map/reshape | solution.py:51
  60.4 23.7 %fusion.47 = f32[4,8,512,512]{2,3,1,0:T(8,128)} fusion(bf16[512,4,8,32]{3,2,1,0:T(8,128)(2,1)} %reshape.294, bf16[512,4,8,32]{3,2,1,0:T(8,128)(2,1)} %reshape.293), kind=kOutput, calls=%fused_computation.72 | convolution fusion | flops 536870912 | bytes 35651584 | tf_op jit(solution)/shard_map/sihd,tihd->ihst/dot_general | solution.py:53
  84.1 35.2 %fusion.72 = (f32[4,8,512]{2,1,0:T(8,128)S(1)}, f32[4,8,512,512]{2,3,1,0:T(8,128)}) fusion(f32[4,8,512,512]{2,3,1,0:T(8,128)} %fusion.47), kind=kOutput, calls=%fused_computation.121 | output fusion | flops 33554944 | bytes 67174400 | tf_op jit(solution)/shard_map/sub | solution.py:56
  119.3 1.7 convolution_convert_fusion.2
  121.0 5.8 %reshape.292 = bf16[512,4,8,32]{3,2,1,0:T(8,128)(2,1)} reshape(bf16[2048,256]{1,0:T(8,128)(2,1)} %convolution_convert_fusion.2) | data formatting | bytes 2097152 | tf_op jit(solution)/shard_map/reshape | solution.py:52
  126.8 17.7 %fusion.55 = f32[512,4,8,32]{0,3,2,1:T(8,128)} fusion(f32[4,8,512,512]{2,3,1,0:T(8,128)} %get-tuple-element.315, f32[4,8,512]{2,1,0:T(8,128)S(1)} %get-tuple-element.314, bf16[512,4,8,32]{3,2,1,0:T(8,128)(2,1)} %reshape.292), kind=kOutput, calls=%fused_computation.95 | convolution fusion | flops 553648128 | bytes 36765696 | tf_op jit(solution)/shard_map/ihst,tihd->sihd/dot_general | solution.py:57
  144.4 8.4 %copy.95 = f32[512,4,8,32]{3,2,1,0:T(8,128)} copy(f32[512,4,8,32]{0,3,2,1:T(8,128)} %fusion.55) | data formatting | bytes 4194304 | tf_op jit(solution)/shard_map/ihst,tihd->sihd/transpose | solution.py:57
  152.8 7.1 %reshape.295 = f32[2048,256]{1,0:T(8,128)} reshape(f32[512,4,8,32]{3,2,1,0:T(8,128)} %copy.95) | data formatting | bytes 4194304 | tf_op jit(solution)/shard_map/reshape | solution.py:59
  159.9 3.9 fusion.73
  163.8 2.3 multiply_reduce_fusion.4
  166.1 4.8 fusion.74
  172.3 3.1 multiply_convert_fusion.8
  178.9 43.8 %all-gather.7.cloned.1.call-done = bf16[512,64,32]{0,2,1:T(8,128)(2,1)} async-done(((bf16[512,4,32]{0,2,1:T(8,128)(2,1)}), bf16[512,64,32]{0,2,1:T(8,128)(2,1)}) %all-gather.7.cloned.1.call-update) | async-done | bytes 2097168 | tf_op jit(solution)/shard_map/all_gather | solution.py:213
  222.8 2.3 dynamic-slice_select_fusion.1
  225.0 47.7 %all-gather.5.cloned.1.call-done = bf16[512,64,32]{0,2,1:T(8,128)(2,1)} async-done(((bf16[512,4,32]{0,2,1:T(8,128)(2,1)}), bf16[512,64,32]{0,2,1:T(8,128)(2,1)}) %all-gather.5.cloned.1.call-update) | async-done | bytes 2097168 | tf_op jit(solution)/shard_map/all_gather | solution.py:212
  272.8 2.3 dynamic-slice_select_fusion
  275.3 18.4 %all-gather = bf16[16,4,128]{2,1,0:T(4,128)(2,1)S(1)} all-gather(bf16[1,4,128]{2,1,0:T(4,128)(2,1)S(1)} %fusion.58), channel_id=1, replica_groups=mesh['row'=8,'col'=16] {'col'}, dimensions={0}, use_global_device_ids=true | all-gather | bytes 17408 | tf_op jit(solution)/shard_map/all_gather | solution.py:214
  293.8 21.8 %all-gather.1 = bf16[16,4,128]{2,1,0:T(4,128)(2,1)S(1)} all-gather(bf16[1,4,128]{2,1,0:T(4,128)(2,1)S(1)} %fusion.59), channel_id=1, replica_groups=mesh['row'=8,'col'=16] {'col'}, dimensions={0}, use_global_device_ids=true | all-gather | bytes 17408 | tf_op jit(solution)/shard_map/all_gather | solution.py:215
  315.6 26.7 %all-reduce = (bf16[32,128]{1,0:T(8,128)(2,1)S(1)}, bf16[2,16,128]{2,1,0:T(8,128)(2,1)S(1)}) all-reduce(bf16[32,128]{1,0:T(8,128)(2,1)S(1)} %dynamic-slice_select_fusion.3, bf16[2,16,128]{2,1,0:T(8,128)(2,1)S(1)} %bitcast.208), channel_id=1, replica_groups=mesh['row'=8,'col'=16] {'row'}, use_global_device_ids=true, to_apply=%region_9.10 | all-reduce | flops 8192 | bytes 32768 | tf_op jit(solution)/shard_map/psum | solution.py:15
  342.3 1.1 convert_element_type.154
  343.4 34.9 %all-reduce.4.cloned.1.call-done = (bf16[512,1024]{0,1:T(8,128)(2,1)}, bf16[2,512,16,32]{1,3,2,0:T(8,128)(2,1)}) async-done(((bf16[512,1024]{0,1:T(8,128)(2,1)}, bf16[2,512,16,32]{1,3,2,0:T(8,128)(2,1)}), (bf16[512,1024]{0,1:T(8,128)(2,1)}, bf16[2,512,16,32]{1,3,2,0:T(8,128)(2,1)})) %all-reduce.4.cloned.1.call-update) | async-done | bytes 2097168 | tf_op jit(solution)/shard_map/psum | solution.py:15
  378.3 43.3 %while.25 = (s32[]{:T(128)}, f32[2,16,64,64]{3,1,0,2:T(8,128)}, bf16[2,16,128]{2,1,0:T(8,128)(2,1)S(1)}, bf16[64,128]{1,0:T(8,128)(2,1)S(1)}, s32[2]{0:T(128)S(1...) while((s32[]{:T(128)}, f32[2,16,64,64]{3,1,0,2:T(8,128)}, ...), condition=%wide.region_19.20_spmd.clone, body=%wide.region_16.19_spmd.clone.sunk | while | flops 1649228800 | bytes 28788408 | solution.py:139
  379.9 5.4 %fusion.160 = bf16[16,64,32,32]{1,2,3,0:T(8,128)(2,1)S(1)} fusion(bf16[64,32,512]{2,1,0:T(8,128)(2,1)} %bitcast.205, bf16[2,512,16,32]{1,3,2,0:T(8,128)(2,1)} %get-tuple-element.594, s32[]{:T(128)} %get-tuple-element.571), kind=kOutput, calls=%fused_computation.34.clone.1 | convolution fusion | flops 1075838976 | bytes 4719104 | tf_op jit(solution)/shard_map/while/body/eval_jaxpr/dot_general | solution.py:101
  385.3 4.6 copy.132
  390.0 5.5 %convert_element_type.275 = bf16[1024,1024]{0,1:T(8,128)(2,1)S(1)} reshape(bf16[16,64,32,32]{1,0,3,2:T(8,128)(2,1)} %copy.132) | data formatting | bytes 4194304 | tf_op jit(solution)/shard_map/while/body/eval_jaxpr/convert_element_type | solution.py:112
  396.3 1.0 fusion.162
  398.9 1.0 copy-done.9
  401.6 5.4 %fusion.160 = bf16[16,64,32,32]{1,2,3,0:T(8,128)(2,1)S(1)} fusion(bf16[64,32,512]{2,1,0:T(8,128)(2,1)} %bitcast.205, bf16[2,512,16,32]{1,3,2,0:T(8,128)(2,1)} %get-tuple-element.594, s32[]{:T(128)} %get-tuple-element.571), kind=kOutput, calls=%fused_computation.34.clone.1 | convolution fusion | flops 1075838976 | bytes 4719104 | tf_op jit(solution)/shard_map/while/body/eval_jaxpr/dot_general | solution.py:101
  407.0 4.6 copy.132
  411.6 5.5 %convert_element_type.275 = bf16[1024,1024]{0,1:T(8,128)(2,1)S(1)} reshape(bf16[16,64,32,32]{1,0,3,2:T(8,128)(2,1)} %copy.132) | data formatting | bytes 4194304 | tf_op jit(solution)/shard_map/while/body/eval_jaxpr/convert_element_type | solution.py:112
  417.9 1.0 fusion.162
  420.5 1.0 copy-done.9
  421.6 50.7 %while.24 = (s32[]{:T(128)}, bf16[2,32,32,128]{3,2,1,0:T(8,128)(2,1)S(1)}, f32[2,32,32,64]{3,2,1,0:T(8,128)}, bf16[2,32,128]{2,1,0:T(8,128)(2,1)S(1)}, bf16[32,1...) while((s32[]{:T(128)}, ...), condition=%wide.region_13.14_spmd.clone, body=%wide.region_10.13_spmd.clone.sunk | while | flops 1649226752 | bytes 22476356 | solution.py:139
  423.4 8.1 %fusion.146 = bf16[32,32,32,32]{3,2,1,0:T(8,128)(2,1)} fusion(bf16[32,32,512,1]{2,1,0,3:T(8,128)(2,1)} %bitcast.209, bf16[2,512,32,32]{1,3,2,0:T(8,128)(2,1)} %get-tuple-element.546, s32[]{:T(128)} %get-tuple-element.521), kind=kOutput, calls=%fused_computation.5.clone.1 | convolution fusion | flops 1075838976 | bytes 4194816 | tf_op jit(solution)/shard_map/while/body/eval_jaxpr/dot_general | solution.py:101
  431.4 11.3 %convert_element_type.269 = bf16[1024,1024]{1,0:T(8,128)(2,1)S(1)} reshape(bf16[32,32,32,32]{3,2,1,0:T(8,128)(2,1)} %fusion.146) | data formatting | bytes 4194304 | tf_op jit(solution)/shard_map/while/body/eval_jaxpr/convert_element_type | solution.py:112
  443.6 1.0 fusion.148
  448.6 8.1 %fusion.146 = bf16[32,32,32,32]{3,2,1,0:T(8,128)(2,1)} fusion(bf16[32,32,512,1]{2,1,0,3:T(8,128)(2,1)} %bitcast.209, bf16[2,512,32,32]{1,3,2,0:T(8,128)(2,1)} %get-tuple-element.546, s32[]{:T(128)} %get-tuple-element.521), kind=kOutput, calls=%fused_computation.5.clone.1 | convolution fusion | flops 1075838976 | bytes 4194816 | tf_op jit(solution)/shard_map/while/body/eval_jaxpr/dot_general | solution.py:101
  456.6 11.3 %convert_element_type.269 = bf16[1024,1024]{1,0:T(8,128)(2,1)S(1)} reshape(bf16[32,32,32,32]{3,2,1,0:T(8,128)(2,1)} %fusion.146) | data formatting | bytes 4194304 | tf_op jit(solution)/shard_map/while/body/eval_jaxpr/convert_element_type | solution.py:112
  468.8 1.0 fusion.148
  472.3 2.8 fusion.61
  (178 shorter events, 21.5 us)
Async XLA Ops:
  7.2 159.0 %copy-start = (bf16[1024,256]{1,0:T(8,128)(2,1)S(1)}, bf16[1024,256]{1,0:T(8,128)(2,1)}, u32[]{:S(2)}) copy-start(bf16[1024,256]{1,0:T(8,128)(2,1)} %param.30) | copy-start | bytes 1572868
  7.2 215.6 %all-gather.7.cloned.1.call-start = ((), (), s32[]{:S(2)}) async-start(), calls=%async_computation.2 | async-start | bytes 2228224 | tf_op jit(solution)/shard_map/all_gather | solution.py:213
  42.9 2.0 copy-start.10
  46.6 5.8 %copy-start.11 = (bf16[256,256]{1,0:T(8,128)(2,1)S(1)}, bf16[256,256]{1,0:T(8,128)(2,1)}, u32[]{:S(2)}) copy-start(bf16[256,256]{1,0:T(8,128)(2,1)} %param.25) | copy-start | bytes 393220
  84.1 35.2 %copy-start.12 = (bf16[256,256]{1,0:T(8,128)(2,1)S(1)}, bf16[256,256]{1,0:T(8,128)(2,1)}, u32[]{:S(2)}) copy-start(bf16[256,256]{1,0:T(8,128)(2,1)} %param.26) | copy-start | bytes 393220
  152.8 7.1 %copy-start.20 = (bf16[256,256]{1,0:T(8,128)(2,1)S(1)}, bf16[256,256]{1,0:T(8,128)(2,1)}, u32[]{:S(2)}) copy-start(bf16[256,256]{1,0:T(8,128)(2,1)} %param.28) | copy-start | bytes 393220
  152.8 7.1 %copy-start.21 = (bf16[256,256]{1,0:T(8,128)(2,1)S(1)}, bf16[256,256]{1,0:T(8,128)(2,1)}, u32[]{:S(2)}) copy-start(bf16[256,256]{1,0:T(8,128)(2,1)} %param.27) | copy-start | bytes 393220
  163.8 2.3 copy-start.18
  170.9 1.4 copy-start.3
  172.3 3.1 copy-start.15
  175.4 1.7 copy-start.16
  177.1 95.7 %all-gather.5.cloned.1.call-start = ((), (), s32[]{:S(2)}) async-start(), calls=%async_computation.1 | async-start | bytes 2228224 | tf_op jit(solution)/shard_map/all_gather | solution.py:212
  178.9 199.4 %all-reduce.4.cloned.1.call-start = ((), (), s32[]{:S(2)}) async-start(), calls=%async_computation.3 | async-start | bytes 4194304 | tf_op jit(solution)/shard_map/psum | solution.py:15
  225.0 50.1 %copy-start.13 = (bf16[256,128]{1,0:T(8,128)(2,1)S(1)}, bf16[256,128]{1,0:T(8,128)(2,1)}, u32[]{:S(2)}) copy-start(bf16[256,128]{1,0:T(8,128)(2,1)} %param.34) | copy-start | bytes 196612
  225.0 50.1 %copy-start.17 = (bf16[4,256]{1,0:T(4,128)(2,1)S(1)}, bf16[4,256]{1,0:T(4,128)(2,1)}, u32[]{:S(2)}) copy-start(bf16[4,256]{1,0:T(4,128)(2,1)} %param.23) | copy-start | bytes 6148
  225.0 68.6 %copy-start.14 = (bf16[256,128]{1,0:T(8,128)(2,1)S(1)}, bf16[256,128]{1,0:T(8,128)(2,1)}, u32[]{:S(2)}) copy-start(bf16[256,128]{1,0:T(8,128)(2,1)} %param.35) | copy-start | bytes 196612
  275.1 103.2 %copy-start.2 = (bf16[1024,128]{1,0:T(8,128)(2,1)S(1)}, bf16[1024,128]{1,0:T(8,128)(2,1)}, u32[]{:S(2)}) copy-start(bf16[1024,128]{1,0:T(8,128)(2,1)} %param.33) | copy-start | bytes 786436
  275.1 103.2 %copy-start.4 = (bf16[65,128]{1,0:T(8,128)(2,1)S(1)}, bf16[65,128]{1,0:T(8,128)(2,1)}, u32[]{:S(2)}) copy-start(bf16[65,128]{1,0:T(8,128)(2,1)} %param.36) | copy-start | bytes 49924
  275.1 103.2 %copy-start.5 = (bf16[128,64]{0,1:T(8,128)(2,1)S(1)}, bf16[128,64]{0,1:T(8,128)(2,1)}, u32[]{:S(2)}) copy-start(bf16[128,64]{0,1:T(8,128)(2,1)} %param.39) | copy-start | bytes 49156
  395.9 1.4 copy-start.22
  396.0 1.4 copy-start.24
  397.3 1.5 copy-start.8
  398.9 1.1 copy-start.9
  417.6 1.4 copy-start.22
  417.6 1.4 copy-start.24
  419.0 1.5 copy-start.8
  420.5 1.1 copy-start.9
  443.5 1.6 copy-start.23
  443.5 1.6 copy-start.25
  443.6 2.4 copy-start.6
  446.1 1.0 copy-start.7
  468.7 1.6 copy-start.23
  468.7 1.6 copy-start.25
  468.8 2.4 copy-start.6
  471.3 1.0 copy-start.7
  472.3 2.8 copy-start.19
  472.3 2.8 copy-start.1
Sparse Core Ops, SparseCore 0:
  177.2 45.4 all-gather.6
  225.8 46.9 all-gather.4
  275.3 102.8 all-reduce.3
where the time goes:
time: 491 us; the launch traced here: 482 us
  waiting for transfers between devices  126 us (26%)
  blocking collectives  95.1 us (19%)
  local copies, waits for them, and re-layouts  94.6 us (19%)
  matrix products  93.4 us (19%)
  other arithmetic  54.1 us (11%)
  between operations  14.5 us (3%)
    all_gather x1, waiting for transfers between devices, shards(): lax.all_gather(left_opm, 'col', axis=1, tiled=True)  47.7 us
    all_gather x1, waiting for transfers between devices, shards(): lax.all_gather(right_opm, 'col', axis=1, tiled=True)  43.8 us
    convert_element_type x6, local copies, waits for them, and re-layouts, one_block(): outer = (outer / count_seq).astype(jnp.bfloat16)  42.8 us
    sub x1, other arithmetic, alignment_layer(): weights = jax.nn.softmax(scores, -1).astype(jnp.bfloat16)  35.2 us
    psum x1, waiting for transfers between devices, spread_2(): return lax.psum(block, axis)  34.9 us
    all_to_all x1, blocking collectives, shards(): lax.all_to_all(fragment_collection, ('row', 'col'), split_axis=2, concat_...  28.2 us
    dot_general x4, matrix products, one_block(): lax.dot_general(a_blk.reshape(count_seq, step_rows * factor), flat_v, (((...  27 us
    psum x1, blocking collectives, spread_2(): return lax.psum(block, axis)  26.7 us
  transfers between devices with their start and end apart: 3, of which 3 were waited for; matrix products, arithmetic and copies ran while one was open for 1% of the time, Pallas kernels for 0%

commit v1 on v0

v1 whole, which is shorter than its diff:
```python
import functools
import math

import jax
import jax.numpy as jnp
from jax import lax
from jax.experimental import pallas as pl
from jax.experimental.pallas import tpu as pltpu
from jax.sharding import PartitionSpec as P

HEADS = 8
HEAD = 32
CLIP = 32
MESH = pl.DeviceIdType.MESH
FULL = pl.BlockSpec(memory_space=pltpu.VMEM)


def standardize_features(values):
    middle = jnp.mean(values, -1, keepdims=True)
    centred = values - middle
    spread = jnp.mean(centred * centred, -1, keepdims=True)
    return centred * lax.rsqrt(spread + 1e-05)


def mm(a, b):
    return jnp.dot(a, b, preferred_element_type=jnp.float32)


def column_attention(
    x_ref,
    feat_ref,
    wq_ref,
    wk_ref,
    wv_ref,
    wg_ref,
    wo_ref,
    we_ref,
    ws_ref,
    factor_ref,
    row_ref,
    column_ref,
    out_ref,
    a_ref,
    b_ref,
    q_scr,
    kt_scr,
    v_scr,
    acc_scr,
    fac_scr,
):
    step = pl.program_id(0)
    seqs = x_ref.shape[1]
    x = x_ref[0].astype(jnp.float32)
    normed = standardize_features(x).astype(jnp.bfloat16)
    q_scr[...] = mm(normed, wq_ref[...]).astype(jnp.bfloat16)
    kt_scr[...] = mm(normed, wk_ref[...]).T.astype(jnp.bfloat16)
    v = mm(normed, wv_ref[...]).astype(jnp.bfloat16)
    ones = jnp.ones((seqs, 128), jnp.bfloat16)
    v_scr[0] = jnp.concatenate([v[:, :128], ones], axis=1)
    v_scr[1] = jnp.concatenate([v[:, 128:], ones], axis=1)
    acc_scr[...] = jnp.zeros_like(acc_scr)
    lane = lax.broadcasted_iota(jnp.int32, (seqs, 256), 1)
    factor = math.log2(math.e) / math.sqrt(HEAD)

    def one_head(h, carry):
        group = h // 4
        q = jnp.where(lane // HEAD == h, q_scr[...], jnp.zeros((), jnp.bfloat16))
        scores = mm(q, kt_scr[...])
        top = jnp.max(scores, axis=-1, keepdims=True)
        weights = jnp.exp2((scores - top) * factor).astype(jnp.bfloat16)
        values = jnp.where(
            lane % 128 // HEAD == h % 4, v_scr[group], jnp.zeros((), jnp.bfloat16)
        )
        acc_scr[group] += mm(weights, values)
        return carry

    lax.fori_loop(0, HEADS, one_head, 0)
    attended = jnp.concatenate(
        [
            acc_scr[0, :, :128] / acc_scr[0, :, 128:],
            acc_scr[1, :, :128] / acc_scr[1, :, 128:],
        ],
        axis=1,
    )
    gate = jax.nn.sigmoid(mm(normed, wg_ref[...]))
    mixed = (attended * gate).astype(jnp.bfloat16)
    first = x + mm(mixed, wo_ref[...])
    hidden = jnp.maximum(
        mm(standardize_features(first).astype(jnp.bfloat16), we_ref[...]), 0.0
    ).astype(jnp.bfloat16)
    second = first + mm(hidden, ws_ref[...])
    out_ref[...] = second.astype(jnp.bfloat16)
    factors = mm(standardize_features(second).astype(jnp.bfloat16), factor_ref[...])
    fac_scr[...] = jnp.where(lane % 128 // HEAD == step, factors, fac_scr[...])

    @pl.when(step == pl.num_programs(0) - 1)
    def _():
        a_ref[:seqs, :] = fac_scr[:, :128].astype(jnp.bfloat16)
        b_ref[:128, :] = fac_scr[:, 128:].T.astype(jnp.bfloat16)
        feat = feat_ref[...]
        a_ref[seqs:, :] = mm(feat, row_ref[...]).astype(jnp.bfloat16)
        b_ref[128:, :128] = mm(feat, column_ref[...]).astype(jnp.bfloat16)
        b_ref[128:, 128:] = jnp.zeros((16, seqs - 128), jnp.bfloat16)


def run_attention(x, feat, weights, interpret=False):
    count_res, seqs, width = x.shape
    whole = [FULL] * (1 + len(weights))
    return pl.pallas_call(
        column_attention,
        grid=(count_res,),
        in_specs=[pl.BlockSpec((1, seqs, width), lambda i: (i, 0, 0))] + whole,
        out_specs=[
            pl.BlockSpec((seqs, width), lambda i: (0, i)),
            pl.BlockSpec((seqs + 16, 128), lambda i: (0, 0)),
            pl.BlockSpec((144, seqs), lambda i: (0, 0)),
        ],
        out_shape=[
            jax.ShapeDtypeStruct((seqs, count_res * width), jnp.bfloat16),
            jax.ShapeDtypeStruct((seqs + 16, 128), jnp.bfloat16),
            jax.ShapeDtypeStruct((144, seqs), jnp.bfloat16),
        ],
        scratch_shapes=[
            pltpu.VMEM((seqs, width), jnp.bfloat16),
            pltpu.VMEM((width, seqs), jnp.bfloat16),
            pltpu.VMEM((2, seqs, width), jnp.bfloat16),
            pltpu.VMEM((2, seqs, width), jnp.float32),
            pltpu.VMEM((seqs, width), jnp.float32),
        ],
        compiler_params=pltpu.CompilerParams(
            dimension_semantics=("arbitrary",), vmem_limit_bytes=48 * 1024 * 1024
        ),
        name="column_attention",
    )(x, feat, *weights)


def spread_factors(a_ref, b_ref, a_all, b_all, a_send, a_recv, b_send, b_recv):
    rows, cols = lax.axis_size("row"), lax.axis_size("col")
    r, c = lax.axis_index("row"), lax.axis_index("col")
    half = cols // 2
    dest = 2 * r + c // half
    slot = c % half
    source_row = c // 2
    source_col = c % 2 * half
    barrier = pltpu.get_barrier_semaphore()
    for k in range(1, cols):
        pl.semaphore_signal(
            barrier, inc=1, device_id=(r, (c + k) % cols), device_id_type=MESH
        )
    for k in range(rows):

        @pl.when(jnp.logical_or(k != 0, dest != c))
        def _(k=k):
            pl.semaphore_signal(
                barrier, inc=1, device_id=((r + k) % rows, dest), device_id_type=MESH
            )

    for d in range(half):

        @pl.when(jnp.logical_or(source_row != r, source_col + d != c))
        def _(d=d):
            pl.semaphore_signal(
                barrier, inc=1, device_id=(source_row, source_col + d), device_id_type=MESH
            )

    own = jnp.where(dest == c, 1, 0)
    pl.semaphore_wait(barrier, cols - 1 + rows + half - 2 * own)

    def a_copy(k):
        return pltpu.make_async_remote_copy(
            src_ref=a_ref,
            dst_ref=a_all.at[c],
            send_sem=a_send.at[k],
            recv_sem=a_recv.at[c],
            device_id=(r, (c + k) % cols),
            device_id_type=MESH,
        )

    def b_copy(k):
        return pltpu.make_async_remote_copy(
            src_ref=b_ref,
            dst_ref=b_all.at[slot],
            send_sem=b_send.at[k],
            recv_sem=b_recv.at[slot],
            device_id=((r + k) % rows, dest),
            device_id_type=MESH,
        )

    def landed(ref, sem):
        return pltpu.make_async_remote_copy(
            src_ref=ref,
            dst_ref=ref,
            send_sem=sem,
            recv_sem=sem,
            device_id=(r, c),
            device_id_type=MESH,
        )

    for k in range(max(cols, rows)):
        if 0 < k < rows:
            b_copy(k).start()
        if k == 0:

            @pl.when(dest != c)
            def _():
                b_copy(0).start()

        if k > 0:
            a_copy(k).start()
    a_all[c] = a_ref[...]

    @pl.when(dest == c)
    def _():
        b_all[slot] = b_ref[...]

    for k in range(1, cols):
        a_copy(k).wait_send()
    for k in range(1, rows):
        b_copy(k).wait_send()

    @pl.when(dest != c)
    def _():
        b_copy(0).wait_send()

    for k in range(1, cols):
        origin = (c + k) % cols
        landed(a_all.at[origin], a_recv.at[origin]).wait_recv()
    for d in range(half):

        @pl.when(jnp.logical_or(source_row != r, source_col + d != c))
        def _(d=d):
            landed(b_all.at[d], b_recv.at[d]).wait_recv()


def run_spread(a_block, b_block, rows, cols):
    half = cols // 2
    return pl.pallas_call(
        spread_factors,
        in_specs=[FULL, FULL],
        out_specs=[FULL, FULL],
        out_shape=[
            jax.ShapeDtypeStruct((cols,) + a_block.shape, jnp.bfloat16),
            jax.ShapeDtypeStruct((half,) + b_block.shape, jnp.bfloat16),
        ],
        scratch_shapes=[
            pltpu.SemaphoreType.DMA((cols,)),
            pltpu.SemaphoreType.DMA((cols,)),
            pltpu.SemaphoreType.DMA((rows,)),
            pltpu.SemaphoreType.DMA((half,)),
        ],
        compiler_params=pltpu.CompilerParams(collective_id=0, has_side_effects=True),
        name="spread_factors",
    )(a_block, b_block)


def pair_tile(
    pos_ref,
    a_ref,
    b_ref,
    offset_ref,
    project_ref,
    expand_ref,
    shrink_ref,
    bins_ref,
    pair_ref,
    logit_ref,
    c_scr,
    x_scr,
    right_scr,
):
    step = pl.program_id(0)
    seqs = b_ref.shape[2]

    @pl.when(step == 0)
    def _():
        for d in range(8):
            right_scr[4 * d : 4 * d + 4, :] = b_ref[d, 128:, :128].astype(jnp.float32)[:4]

    factors = jnp.concatenate([a_ref[0, :seqs, :], a_ref[1, :seqs, :]], axis=1)
    outer = mm(b_ref[:, :128, :].reshape(1024, seqs), factors)
    c_scr[0] = outer[:, :128]
    c_scr[1] = outer[:, 128:]
    lane = lax.broadcasted_iota(jnp.int32, (32, 128), 1)
    low = lane < 64
    even = lane % 64 < 32
    for part in range(2):
        for e in range(0, 32, 4):
            y = [c_scr[part, pl.ds(e + k, 32, stride=32), :] for k in range(4)]
            u = [
                jnp.where(low, y[0], pltpu.roll(y[2], 64, 1)),
                jnp.where(low, y[1], pltpu.roll(y[3], 64, 1)),
                jnp.where(low, pltpu.roll(y[0], 64, 1), y[2]),
                jnp.where(low, pltpu.roll(y[1], 64, 1), y[3]),
            ]
            z = [
                jnp.where(even, u[0], pltpu.roll(u[1], 32, 1)),
                jnp.where(even, pltpu.roll(u[0], 96, 1), u[1]),
                jnp.where(even, u[2], pltpu.roll(u[3], 32, 1)),
                jnp.where(even, pltpu.roll(u[2], 96, 1), u[3]),
            ]
            for i in range(4):
                row = (part * 4 + i) * 32
                x_scr[row : row + 32, e * 32 : e * 32 + 128] = (z[i] * (1.0 / seqs)).astype(
                    jnp.bfloat16
                )
    projected = mm(x_scr[...], project_ref[...])
    index = lax.broadcasted_iota(jnp.int32, (256, 128), 0)
    bins = lax.broadcasted_iota(jnp.int32, (256, 128), 1)
    offset = (pos_ref[1] + index % 32) - (pos_ref[0] + step * 8 + index // 32)
    onehot = jnp.where(jnp.clip(offset, -CLIP, CLIP) + CLIP == bins, 1.0, 0.0)
    relative = mm(onehot.astype(jnp.bfloat16), offset_ref[...])
    left0 = a_ref[0, seqs:, :].astype(jnp.float32)
    left1 = a_ref[1, seqs:, :].astype(jnp.float32)
    left = [left0[i : i + 1] for i in range(4)] + [left1[i : i + 1] for i in range(4)]
    right = right_scr[...]
    embedded = jnp.concatenate([right + one for one in left], axis=0)
    start = embedded + relative + projected
    hidden = jnp.maximum(
        mm(standardize_features(start).astype(jnp.bfloat16), expand_ref[...]), 0.0
    ).astype(jnp.bfloat16)
    final = (start + mm(hidden, shrink_ref[...])).astype(jnp.bfloat16)
    pair_ref[...] = final.reshape(8, 32, 128)
    logit_ref[...] = mm(final, bins_ref[...]).reshape(8, 32, 64)


def run_pair(pos, a_all, b_all, offset, project, expand, shrink, bins):
    seqs = b_all.shape[2]
    return pl.pallas_call(
        pair_tile,
        grid=(8,),
        in_specs=[
            pl.BlockSpec(memory_space=pltpu.SMEM),
            pl.BlockSpec((2,) + a_all.shape[1:], lambda i: (i, 0, 0)),
        ]
        + [FULL] * 6,
        out_specs=[
            pl.BlockSpec((8, 32, 128), lambda i: (i, 0, 0)),
            pl.BlockSpec((8, 32, 64), lambda i: (i, 0, 0)),
        ],
        out_shape=[
            jax.ShapeDtypeStruct((64, 32, 128), jnp.bfloat16),
            jax.ShapeDtypeStruct((64, 32, 64), jnp.float32),
        ],
        scratch_shapes=[
            pltpu.VMEM((2, 1024, 128), jnp.float32),
            pltpu.VMEM((256, 1024), jnp.bfloat16),
            pltpu.VMEM((32, 128), jnp.float32),
        ],
        compiler_params=pltpu.CompilerParams(
            dimension_semantics=("arbitrary",), vmem_limit_bytes=48 * 1024 * 1024
        ),
        name="pair_tile",
    )(pos, a_all, b_all, offset, project, expand, shrink, bins)


def shards(
    homolog_stack,
    per_amino_features,
    asking_matrix,
    lookup_matrix,
    content_matrix,
    sigmoid_scaling_matrix,
    attention_result_matrix,
    stack_transition_expand_matrix,
    stack_transition_shrink_matrix,
    former_factor_matrix,
    latter_factor_matrix,
    factor_mean_projection,
    row_amino_embedding,
    column_amino_embedding,
    offset_embedding_matrix,
    grid_transition_expand,
    grid_transition_shrink,
    distance_bins_matrix,
):
    rows = lax.axis_size("row")
    cols = lax.axis_size("col")
    whole = rows * cols
    seq_here, residues, width = homolog_stack.shape
    res_here = residues // whole
    fragments = homolog_stack.reshape(1, seq_here, whole, res_here, width)
    moved = lax.all_to_all(fragments, ("row", "col"), split_axis=2, concat_axis=0, tiled=True)
    local = moved.reshape(-1, res_here, width)
    seqs = local.shape[0]
    both = jnp.concatenate(
        [jnp.tile(former_factor_matrix, (1, 4)), jnp.tile(latter_factor_matrix, (1, 4))], axis=1
    )
    updated, a_block, b_block = run_attention(
        local.transpose(1, 0, 2),
        jnp.pad(per_amino_features, ((0, 12), (0, 0))),
        (
            asking_matrix,
            lookup_matrix,
            content_matrix,
            sigmoid_scaling_matrix,
            attention_result_matrix,
            stack_transition_expand_matrix,
            stack_transition_shrink_matrix,
            both,
            row_amino_embedding,
            column_amino_embedding,
        ),
    )
    alignment_output = updated.reshape(seqs, res_here, width)
    a_all, b_all = run_spread(a_block, b_block, rows, cols)
    r, c = lax.axis_index("row"), lax.axis_index("col")
    factor = former_factor_matrix.shape[1]
    project = (
        factor_mean_projection.reshape(factor, factor, -1)
        .transpose(1, 0, 2)
        .reshape(factor * factor, -1)
    )
    row_len, col_len = residues // rows, residues // cols
    pos = jnp.stack([r * row_len, c * col_len]).astype(jnp.int32)
    pair_output, logits = run_pair(
        pos,
        a_all,
        b_all,
        jnp.pad(offset_embedding_matrix, ((0, 127 - 2 * CLIP), (0, 0))),
        project,
        grid_transition_expand,
        grid_transition_shrink,
        distance_bins_matrix,
    )
    rounded = logits.astype(jnp.bfloat16)
    mirrors = []
    for k in range(2):
        pairs = []
        for rr in range(rows):
            for cc in range(cols):
                pairs.append((rr * cols + cc, cc // 2 * cols + 2 * rr + (cc % 2 ^ k)))
        half = lax.dynamic_slice_in_dim(rounded, (c % 2 ^ k) * col_len, col_len, 0)
        mirrors.append(lax.ppermute(half, ("row", "col"), pairs))
    flip = c % 2 == 0
    first = jnp.where(flip, mirrors[0], mirrors[1])
    second = jnp.where(flip, mirrors[1], mirrors[0])
    mirror = jnp.concatenate([first, second], axis=1)
    distogram = (logits + mirror.transpose(1, 0, 2).astype(jnp.float32)).astype(jnp.bfloat16)
    return (alignment_output, pair_output, distogram)


def solution(mesh):
    placed = (P(("row", "col"), None, None), P(("row", "col"), None)) + (P(),) * 16
    return jax.shard_map(
        shards,
        mesh=mesh,
        in_specs=placed,
        out_specs=(P(None, ("row", "col"), None), P("row", "col", None), P("row", "col", None)),
        check_vma=False,
    )
```

time: 491 us -> 220 us (0.45); the launches traced: 482 us -> 216 us
  Pallas kernels: 0 us -> 138 us
  blocking collectives: 95.1 us -> 0 us
  matrix products: 93.4 us -> 0 us
  waiting for transfers between devices: 126 us -> 36.2 us
  local copies, waits for them, and re-layouts: 94.6 us -> 21.3 us
  other arithmetic: 54.1 us -> 1.09 us
  starting transfers between devices: 0.12 us -> 18.3 us
  between operations: 14.5 us -> 0.92 us
    pallas_call x0 -> x3, Pallas kernels: none -> 138 us  [the longest x1 84.4 us: run_spread(): pl.pallas_call(spread_factors, in_specs=[FULL, FULL], out_specs=[FULL, FU...]
    dot_general x31 -> x0, matrix products: 93.4 us -> none  [the longest x4 27 us: one_block(): lax.dot_general(a_blk.reshape(count_seq, step_rows * factor), flat_v, (((...]
    all_gather x2 -> x0, waiting for transfers between devices: 91.6 us -> none  [the longest x1 47.7 us: shards(): lax.all_gather(left_opm, 'col', axis=1, tiled=True)]
    convert_element_type x10 -> x0, local copies, waits for them, and re-layouts: 46.5 us -> none  [the longest x6 42.8 us: one_block(): outer = (outer / count_seq).astype(jnp.bfloat16)]
    all_gather x2 -> x0, blocking collectives: 40.2 us -> none  [the longest x1 21.8 us: shards(): lax.all_gather(right_pair, 'col', axis=0, tiled=True)]
    sub x1 -> x0, other arithmetic: 35.2 us -> none  [alignment_layer(): weights = jax.nn.softmax(scores, -1).astype(jnp.bfloat16)]
    psum x1 -> x0, waiting for transfers between devices: 34.9 us -> none  [spread_2(): return lax.psum(block, axis)]
    all_to_all x1 -> x0, blocking collectives: 28.2 us -> none  [shards(): lax.all_to_all(fragment_collection, ('row', 'col'), split_axis=2, concat_...]
  transfers between devices with their start and end apart: 3 -> 3, of which waited for: 3 -> 3; matrix products, arithmetic and copies ran while one was open for 1% -> 2% of each run, Pallas kernels for 0% -> 0%
where the time goes in v1:
time: 220 us; the launch traced here: 216 us
  Pallas kernels  138 us (63%)
  waiting for transfers between devices  36.2 us (16%)
  local copies, waits for them, and re-layouts  21.3 us (10%)
  starting transfers between devices  18.3 us (8%)
    pallas_call x1, Pallas kernels, run_spread(): pl.pallas_call(spread_factors, in_specs=[FULL, FULL], out_specs=[FULL, FU...  84.4 us
    pallas_call x1, Pallas kernels, run_attention(): pl.pallas_call(column_attention, grid=(count_res,), in_specs=[pl.BlockSpe...  34.6 us
    ppermute x2, waiting for transfers between devices, shards(): mirrors.append(lax.ppermute(half, ('row', 'col'), pairs))  20.5 us
    pallas_call x1, Pallas kernels, run_pair(): pl.pallas_call(pair_tile, grid=(8,), in_specs=[pl.BlockSpec(memory_space=...  19.4 us
    unnamed x48, local copies, waits for them, and re-layouts  17.5 us
    all_to_all x1, waiting for transfers between devices, shards(): lax.all_to_all(fragments, ('row', 'col'), split_axis=2, concat_axis=0, ti...  15.8 us
    all_to_all x1, starting transfers between devices, shards(): lax.all_to_all(fragments, ('row', 'col'), split_axis=2, concat_axis=0, ti...  10.8 us
    ppermute x2, starting transfers between devices, shards(): mirrors.append(lax.ppermute(half, ('row', 'col'), pairs))  7.51 us
  transfers between devices with their start and end apart: 3, of which 3 were waited for; matrix products, arithmetic and copies ran while one was open for 2% of the time, Pallas kernels for 0%

profile of v1, /device:TPU:7, one launch (start us, length us, event | category | flops | bytes accessed | tf_op | source)
XLA Modules:
  0.0 216.2 jit_solution(3561263432014510215)
XLA Ops:
  0.6 0.0 copy-start.19
  0.6 0.0 copy-start.20
  0.7 0.0 copy-start.22
  0.7 0.0 copy-start.18
  0.7 0.0 copy-start.17
  0.7 0.0 copy-start.21
  0.7 3.0 %copy.33 = bf16[4,512,256]{2,0,1:T(4,128)(2,1)} copy(bf16[4,512,256]{2,1,0:T(8,128)(2,1)} %param.18) | data formatting | bytes 2097152 | tf_op args[0]
  3.7 10.8 %all-to-all-start = ((bf16[1,4,128,4,256]{4,1,3,0,2:T(4,128)(2,1)}), bf16[1,4,128,4,256]{4,1,3,0,2:T(4,128)(2,1)S(1)}, u32[]{:S(2)}, u32[]{:S(2)}) async-start(bf16[1,4,128,4,256]{4,1,3,0,2:T(4,128)(2,1)} %bitcast), calls=%async_computation | async-start | bytes 2097152 | tf_op jit(solution)/shard_map/all_to_all | solution.py:382
  14.5 0.1 copy.36
  14.7 0.1 copy.35
  14.8 0.6 pad.9.offset_ref
  15.5 0.1 copy.37
  15.6 0.7 copy.38.bins_ref
  16.3 0.1 pad_add_fusion.pos_ref
  16.4 0.0 copy-start.2
  16.4 0.0 copy-start.3
  16.4 15.8 %all-to-all-done = bf16[1,4,128,4,256]{4,1,3,0,2:T(4,128)(2,1)S(1)} async-done(((bf16[1,4,128,4,256]{4,1,3,0,2:T(4,128)(2,1)}), bf16[1,4,128,4,256]{4,1,3,0,2:T(4,128)(2,1)S(1)}, u32[]{:S(2)}, u32[]{:S(2)}) %all-to-all-start) | async-done | bytes 1048608 | tf_op jit(solution)/shard_map/all_to_all | solution.py:382
  32.2 0.4 copy.34
  32.5 0.3 reshape.31
  32.8 0.0 copy-done.2
  32.8 0.0 copy-done.3
  32.8 0.0 copy-start.8
  32.9 0.9 copy-done.8
  33.8 0.9 copy-done.9
  34.7 0.9 copy-done.10
  35.6 0.9 copy-done.11
  36.5 0.9 copy-done.12
  37.4 0.8 copy-done.15
  38.2 0.8 copy-done.16
  39.1 34.6 %column_attention.1 = (bf16[512,1024]{1,0:T(8,128)(2,1)S(1)}, bf16[528,128]{1,0:T(8,128)(2,1)S(1)}, bf16[144,512]{1,0:T(8,128)(2,1)S(1)}) custom-call(bf16[4,512,256]{2,1,0:T(8,128)(2,1)S(1)} %bitcast.19, bf16[16,256]{1,0:T(8,128)(2,1)S(1)} %pad.8.feat_ref, bf16[256,256]{1,0:T(8,128)(2,1)S(1)} %copy-done.8, bf16[256,256]{1,0:T(8,128)(2,1)S(1)} %copy-done.9, ...), custom_call_target="tpu_custom_call" | custom-call | tf_op jit(solution)/shard_map/column_attention/pallas_call | solution.py:109
  73.6 0.0 copy-start.4
  73.6 0.7 copy-done.4
  74.3 0.7 copy-done.5
  74.9 84.4 %spread_factors.1 = (bf16[16,528,128]{2,1,0:T(8,128)(2,1)}, bf16[8,144,512]{2,1,0:T(8,128)(2,1)}) custom-call(bf16[528,128]{1,0:T(8,128)(2,1)} %copy-done.5, bf16[144,512]{1,0:T(8,128)(2,1)} %copy-done.4), custom_call_target="tpu_custom_call" | custom-call | tf_op jit(solution)/shard_map/spread_factors/pallas_call | solution.py:237
  159.4 1.6 copy-done
  161.0 1.3 copy-done.1
  162.2 0.8 copy-done.6
  163.0 0.8 copy-done.7
  163.8 0.9 copy-done.13
  164.7 0.9 copy-done.14
  165.6 19.4 %pair_tile.1 = (bf16[64,32,128]{2,1,0:T(8,128)(2,1)}, f32[64,32,64]{2,1,0:T(8,128)S(1)}) custom-call(s32[2]{0:T(128)S(1)} %pad_add_fusion.pos_ref, bf16[16,528,128]{2,1,0:T(8,128)(2,1)S(1)} %copy-done, bf16[8,144,512]{2,1,0:T(8,128)(2,1)S(1)} %copy-done.1, bf16[128,128]{1,0:T(8,128)(2,1)S(1)} %copy-done.6, bf16[1024,128]{1,0:T(8,128)(2,1)S(1)} %bitcast.20, ...), custom_call_target="tpu_custom_call" | custom-call | tf_op jit(solution)/shard_map/pair_tile/pallas_call | solution.py:328
  185.0 0.6 copy.41
  185.6 1.9 collective-permute-start
  187.5 5.6 %collective-permute-start.1 = (bf16[32,32,64]{2,0,1:T(8,128)(2,1)S(1)}, bf16[32,32,64]{2,0,1:T(8,128)(2,1)S(1)}, u32[]{:S(2)}, u32[]{:S(2)}) collective-permute-start(bf16[32,32,64]{2,0,1:T(8,128)(2,1)S(1)} %get-tuple-element.20), channel_id=1, source_target_pairs={{0,1},{1,0},{2,17},{3,16},{4,33},{5,32},{6,49},{7,48},{8,65},{9,64... | collective-permute-start | bytes 393224 | tf_op jit(solution)/shard_map/ppermute | solution.py:433
  193.1 1.6 reshape.32
  194.7 14.9 %collective-permute-done = bf16[32,32,64]{2,0,1:T(8,128)(2,1)S(1)} collective-permute-done((bf16[32,32,64]{2,0,1:T(8,128)(2,1)S(1)}, bf16[32,32,64]{2,0,1:T(8,128)(2,1)S(1)}, u32[]{:S(2)}, u32[]{:S(2)}) %collective-permute-start) | collective-permute-done | bytes 131104 | tf_op jit(solution)/shard_map/ppermute | solution.py:433
  209.6 5.6 %collective-permute-done.1 = bf16[32,32,64]{2,0,1:T(8,128)(2,1)S(1)} collective-permute-done((bf16[32,32,64]{2,0,1:T(8,128)(2,1)S(1)}, bf16[32,32,64]{2,0,1:T(8,128)(2,1)S(1)}, u32[]{:S(2)}, u32[]{:S(2)}) %collective-permute-start.1) | collective-permute-done | bytes 131104 | tf_op jit(solution)/shard_map/ppermute | solution.py:433
  215.2 1.0 fusion
  (25 shorter events, 0.2 us)
Async XLA Ops:
  0.6 13.9 %copy-start.19 = (bf16[256,32]{0,1:T(8,128)(2,1)S(1)}, bf16[256,32]{0,1:T(8,128)(2,1)}, u32[]{:S(2)}) copy-start(bf16[256,32]{0,1:T(8,128)(2,1)} %param.28) | copy-start | bytes 49156
  0.6 14.0 %copy-start.20 = (bf16[256,32]{0,1:T(8,128)(2,1)S(1)}, bf16[256,32]{0,1:T(8,128)(2,1)}, u32[]{:S(2)}) copy-start(bf16[256,32]{0,1:T(8,128)(2,1)} %param.27) | copy-start | bytes 49156
  0.7 14.2 %copy-start.22 = (bf16[4,256]{1,0:T(4,128)(2,1)S(1)}, bf16[4,256]{1,0:T(4,128)(2,1)}, u32[]{:S(2)}) copy-start(bf16[4,256]{1,0:T(4,128)(2,1)} %param.19) | copy-start | bytes 6148
  0.7 14.2 %copy-start.18 = (bf16[65,128]{1,0:T(8,128)(2,1)S(1)}, bf16[65,128]{1,0:T(8,128)(2,1)}, u32[]{:S(2)}) copy-start(bf16[65,128]{1,0:T(8,128)(2,1)} %param.32) | copy-start | bytes 49924
  0.7 14.8 %copy-start.17 = (bf16[1024,128]{1,0:T(8,128)(2,1)S(1)}, bf16[1024,128]{1,0:T(8,128)(2,1)}, u32[]{:S(2)}) copy-start(bf16[1024,128]{1,0:T(8,128)(2,1)} %param.29) | copy-start | bytes 786436
  0.7 14.9 %copy-start.21 = (bf16[128,64]{0,1:T(8,128)(2,1)S(1)}, bf16[128,64]{0,1:T(8,128)(2,1)}, u32[]{:S(2)}) copy-start(bf16[128,64]{0,1:T(8,128)(2,1)} %param.35) | copy-start | bytes 49156
  3.7 28.4 %all-to-all-start = ((bf16[1,4,128,4,256]{4,1,3,0,2:T(4,128)(2,1)}), bf16[1,4,128,4,256]{4,1,3,0,2:T(4,128)(2,1)S(1)}, u32[]{:S(2)}, u32[]{:S(2)}) async-start(bf16[1,4,128,4,256]{4,1,3,0,2:T(4,128)(2,1)} %bitcast), calls=%async_computation | async-start | bytes 2097152 | tf_op jit(solution)/shard_map/all_to_all | solution.py:382
  16.4 16.4 %copy-start.2 = (bf16[256,1024]{1,0:T(8,128)(2,1)S(1)}, bf16[256,1024]{1,0:T(8,128)(2,1)}, u32[]{:S(2)}) copy-start(bf16[256,1024]{1,0:T(8,128)(2,1)} %we_ref.1) | copy-start | bytes 1572868
  16.4 16.4 %copy-start.3 = (bf16[1024,256]{1,0:T(8,128)(2,1)S(1)}, bf16[1024,256]{1,0:T(8,128)(2,1)}, u32[]{:S(2)}) copy-start(bf16[1024,256]{1,0:T(8,128)(2,1)} %ws_ref.1) | copy-start | bytes 1572868
  32.8 0.9 copy-start.8
  33.8 0.9 copy-start.9
  34.7 0.9 copy-start.10
  35.6 0.9 copy-start.11
  36.5 0.9 copy-start.12
  37.4 0.8 copy-start.15
  38.2 0.8 copy-start.16
  73.6 0.7 copy-start.4
  74.3 0.7 copy-start.5
  159.4 1.6 copy-start
  161.0 1.3 copy-start.1
  162.2 0.8 copy-start.6
  163.0 0.8 copy-start.7
  163.8 0.9 copy-start.13
  164.7 0.9 copy-start.14
  185.6 23.9 %collective-permute-start = (bf16[32,32,64]{2,0,1:T(8,128)(2,1)S(1)}, bf16[32,32,64]{2,0,1:T(8,128)(2,1)S(1)}, u32[]{:S(2)}, u32[]{:S(2)}) collective-permute-start(bf16[32,32,64]{2,0,1:T(8,128)(2,1)S(1)} %get-tuple-element.19), channel_id=1, source_target_pairs={{0,0},{1,1},{2,16},{3,17},{4,32},{5,33},{6,48},{7,49},{8,64},{9,65... | collective-permute-start | bytes 393224 | tf_op jit(solution)/shard_map/ppermute | solution.py:433
  187.5 27.6 %collective-permute-start.1 = (bf16[32,32,64]{2,0,1:T(8,128)(2,1)S(1)}, bf16[32,32,64]{2,0,1:T(8,128)(2,1)S(1)}, u32[]{:S(2)}, u32[]{:S(2)}) collective-permute-start(bf16[32,32,64]{2,0,1:T(8,128)(2,1)S(1)} %get-tuple-element.20), channel_id=1, source_target_pairs={{0,1},{1,0},{2,17},{3,16},{4,33},{5,32},{6,49},{7,48},{8,65},{9,64... | collective-permute-start | bytes 393224 | tf_op jit(solution)/shard_map/ppermute | solution.py:433

commit v2 on v1

--- a/solution.py
+++ b/solution.py
@@ -20,6 +20,10 @@
     centred = values - middle
     spread = jnp.mean(centred * centred, -1, keepdims=True)
     return centred * lax.rsqrt(spread + 1e-05)
+
+
+def resident(shape):
+    return pl.BlockSpec(shape, lambda i: (0,) * len(shape))
 
 
 def mm(a, b):
@@ -105,15 +109,15 @@
 
 def run_attention(x, feat, weights, interpret=False):
     count_res, seqs, width = x.shape
-    whole = [FULL] * (1 + len(weights))
+    whole = [resident(one.shape) for one in (feat,) + weights]
     return pl.pallas_call(
         column_attention,
         grid=(count_res,),
         in_specs=[pl.BlockSpec((1, seqs, width), lambda i: (i, 0, 0))] + whole,
         out_specs=[
             pl.BlockSpec((seqs, width), lambda i: (0, i)),
-            pl.BlockSpec((seqs + 16, 128), lambda i: (0, 0)),
-            pl.BlockSpec((144, seqs), lambda i: (0, 0)),
+            FULL,
+            FULL,
         ],
         out_shape=[
             jax.ShapeDtypeStruct((seqs, count_res * width), jnp.bfloat16),
@@ -136,100 +140,111 @@
 
 def spread_factors(a_ref, b_ref, a_all, b_all, a_send, a_recv, b_send, b_recv):
     rows, cols = lax.axis_size("row"), lax.axis_size("col")
+    half = cols // 2
     r, c = lax.axis_index("row"), lax.axis_index("col")
-    half = cols // 2
-    dest = 2 * r + c // half
-    slot = c % half
-    source_row = c // 2
-    source_col = c % 2 * half
+    high, within = c // half, c % half
+    core = c % 2
+    other_core = c + 1 - 2 * core
+    other_high = (1 - high) * half + within
+    other_row = r + 1 - 2 * (r % 2)
+    ahead = 2 - 4 * core
+
+    def along_x(column, shift):
+        return column // half * half + (column % half + shift + half) % half
+
+    def along_y(row, shift):
+        return (row + shift + rows) % rows
+
+    spot = within + 1 - 2 * (within % 2)
+    first_dest = (spot, 2 * r + high)
+    kept = other_row
+    first_origin = (c // 2, c % 2 * half + kept)
     barrier = pltpu.get_barrier_semaphore()
-    for k in range(1, cols):
-        pl.semaphore_signal(
-            barrier, inc=1, device_id=(r, (c + k) % cols), device_id_type=MESH
-        )
-    for k in range(rows):
-
-        @pl.when(jnp.logical_or(k != 0, dest != c))
-        def _(k=k):
-            pl.semaphore_signal(
-                barrier, inc=1, device_id=((r + k) % rows, dest), device_id_type=MESH
-            )
-
-    for d in range(half):
-
-        @pl.when(jnp.logical_or(source_row != r, source_col + d != c))
-        def _(d=d):
-            pl.semaphore_signal(
-                barrier, inc=1, device_id=(source_row, source_col + d), device_id_type=MESH
-            )
-
-    own = jnp.where(dest == c, 1, 0)
-    pl.semaphore_wait(barrier, cols - 1 + rows + half - 2 * own)
-
-    def a_copy(k):
-        return pltpu.make_async_remote_copy(
-            src_ref=a_ref,
-            dst_ref=a_all.at[c],
-            send_sem=a_send.at[k],
-            recv_sem=a_recv.at[c],
-            device_id=(r, (c + k) % cols),
+    peers = [
+        (r, other_core),
+        (r, other_high),
+        (r, along_x(c, 2)),
+        (r, along_x(c, -2)),
+        (other_row, c),
+        (along_y(r, 2), c),
+        (along_y(r, -2), c),
+        first_dest,
+        first_origin,
+    ]
+    for peer in peers:
+        pl.semaphore_signal(barrier, inc=1, device_id=peer, device_id_type=MESH)
+    pl.semaphore_wait(barrier, len(peers))
+    sent = []
+
+    def send(src, full, slot, sends, recvs, number, device):
+        copy = pltpu.make_async_remote_copy(
+            src_ref=src,
+            dst_ref=full.at[slot],
+            send_sem=sends.at[number],
+            recv_sem=recvs.at[slot],
+            device_id=device,
             device_id_type=MESH,
         )
-
-    def b_copy(k):
-        return pltpu.make_async_remote_copy(
-            src_ref=b_ref,
-            dst_ref=b_all.at[slot],
-            send_sem=b_send.at[k],
-            recv_sem=b_recv.at[slot],
-            device_id=((r + k) % rows, dest),
+        copy.start()
+        sent.append(copy)
+
+    def send_a(src, slot, number, column):
+        send(src, a_all, slot, a_send, a_recv, number, (r, column))
+
+    def send_b(src, slot, number, device):
+        send(src, b_all, slot, b_send, b_recv, number, device)
+
+    def arrived(full, slot, recvs):
+        pltpu.make_async_remote_copy(
+            src_ref=full.at[slot],
+            dst_ref=full.at[slot],
+            send_sem=recvs.at[slot],
+            recv_sem=recvs.at[slot],
+            device_id=(r, other_core),
             device_id_type=MESH,
-        )
-
-    def landed(ref, sem):
-        return pltpu.make_async_remote_copy(
-            src_ref=ref,
-            dst_ref=ref,
-            send_sem=sem,
-            recv_sem=sem,
-            device_id=(r, c),
-            device_id_type=MESH,
-        )
-
-    for k in range(max(cols, rows)):
-        if 0 < k < rows:
-            b_copy(k).start()
-        if k == 0:
-
-            @pl.when(dest != c)
-            def _():
-                b_copy(0).start()
-
-        if k > 0:
-            a_copy(k).start()
+        ).wait_recv()
+
+    send_b(b_ref, within, 0, first_dest)
+    send_a(a_ref, c, 0, other_high)
+    send_a(a_ref, c, 1, along_x(c, ahead))
+    send_a(a_ref, c, 2, along_x(c, -ahead))
+    send_a(a_ref, c, 3, other_core)
     a_all[c] = a_ref[...]
-
-    @pl.when(dest == c)
-    def _():
-        b_all[slot] = b_ref[...]
-
-    for k in range(1, cols):
-        a_copy(k).wait_send()
-    for k in range(1, rows):
-        b_copy(k).wait_send()
-
-    @pl.when(dest != c)
-    def _():
-        b_copy(0).wait_send()
-
-    for k in range(1, cols):
-        origin = (c + k) % cols
-        landed(a_all.at[origin], a_recv.at[origin]).wait_recv()
-    for d in range(half):
-
-        @pl.when(jnp.logical_or(source_row != r, source_col + d != c))
-        def _(d=d):
-            landed(b_all.at[d], b_recv.at[d]).wait_recv()
+    arrived(b_all, kept, b_recv)
+    send_b(b_all.at[kept], kept, 1, (other_row, c))
+    send_b(b_all.at[kept], kept, 2, (along_y(r, ahead), c))
+    send_b(b_all.at[kept], kept, 3, (along_y(r, -ahead), c))
+    arrived(a_all, other_high, a_recv)
+    send_a(a_all.at[other_high], other_high, 4, along_x(c, ahead))
+    send_a(a_all.at[other_high], other_high, 5, along_x(c, -ahead))
+    send_a(a_all.at[other_high], other_high, 6, other_core)
+    arrived(b_all, r, b_recv)
+    send_b(b_all.at[r], r, 4, (along_y(r, ahead), c))
+    send_b(b_all.at[r], r, 5, (along_y(r, -ahead), c))
+    for turn, (a_slot, b_slot) in enumerate(((c, kept), (other_high, r))):
+        back = along_x(a_slot, -ahead)
+        arrived(a_all, back, a_recv)
+        send_a(a_all.at[back], back, 7 + 4 * turn, along_x(c, ahead))
+        send_a(a_all.at[back], back, 8 + 4 * turn, other_core)
+        behind = along_y(b_slot, -ahead)
+        arrived(b_all, behind, b_recv)
+        send_b(b_all.at[behind], behind, 6 + turn, (along_y(r, ahead), c))
+        front = along_x(a_slot, ahead)
+        arrived(a_all, front, a_recv)
+        send_a(a_all.at[front], front, 9 + 4 * turn, other_core)
+    for turn, a_slot in enumerate((c, other_high)):
+        far = along_x(a_slot, 4)
+        arrived(a_all, far, a_recv)
+        send_a(a_all.at[far], far, 10 + 4 * turn, other_core)
+    for b_slot in (kept, r):
+        arrived(b_all, along_y(b_slot, ahead), b_recv)
+        arrived(b_all, along_y(b_slot, 4), b_recv)
+    for a_slot in (c, other_high):
+        mate = a_slot + 1 - 2 * core
+        for shift in range(0, half, 2):
+            arrived(a_all, along_x(mate, shift), a_recv)
+    for copy in sent:
+        copy.wait_send()
 
 
 def run_spread(a_block, b_block, rows, cols):
@@ -243,9 +258,9 @@
             jax.ShapeDtypeStruct((half,) + b_block.shape, jnp.bfloat16),
         ],
         scratch_shapes=[
+            pltpu.SemaphoreType.DMA((15,)),
             pltpu.SemaphoreType.DMA((cols,)),
-            pltpu.SemaphoreType.DMA((cols,)),
-            pltpu.SemaphoreType.DMA((rows,)),
+            pltpu.SemaphoreType.DMA((8,)),
             pltpu.SemaphoreType.DMA((half,)),
         ],
         compiler_params=pltpu.CompilerParams(collective_id=0, has_side_effects=True),
@@ -276,7 +291,7 @@
         for d in range(8):
             right_scr[4 * d : 4 * d + 4, :] = b_ref[d, 128:, :128].astype(jnp.float32)[:4]
 
-    factors = jnp.concatenate([a_ref[0, :seqs, :], a_ref[1, :seqs, :]], axis=1)
+    factors = jnp.concatenate([a_ref[2 * step, :seqs, :], a_ref[2 * step + 1, :seqs, :]], axis=1)
     outer = mm(b_ref[:, :128, :].reshape(1024, seqs), factors)
     c_scr[0] = outer[:, :128]
     c_scr[1] = outer[:, 128:]
@@ -309,8 +324,8 @@
     offset = (pos_ref[1] + index % 32) - (pos_ref[0] + step * 8 + index // 32)
     onehot = jnp.where(jnp.clip(offset, -CLIP, CLIP) + CLIP == bins, 1.0, 0.0)
     relative = mm(onehot.astype(jnp.bfloat16), offset_ref[...])
-    left0 = a_ref[0, seqs:, :].astype(jnp.float32)
-    left1 = a_ref[1, seqs:, :].astype(jnp.float32)
+    left0 = a_ref[2 * step, seqs:, :].astype(jnp.float32)
+    left1 = a_ref[2 * step + 1, seqs:, :].astype(jnp.float32)
     left = [left0[i : i + 1] for i in range(4)] + [left1[i : i + 1] for i in range(4)]
     right = right_scr[...]
     embedded = jnp.concatenate([right + one for one in left], axis=0)
@@ -330,9 +345,10 @@
         grid=(8,),
         in_specs=[
             pl.BlockSpec(memory_space=pltpu.SMEM),
-            pl.BlockSpec((2,) + a_all.shape[1:], lambda i: (i, 0, 0)),
+            FULL,
+            FULL,
         ]
-        + [FULL] * 6,
+        + [resident(one.shape) for one in (offset, project, expand, shrink, bins)],
         out_specs=[
             pl.BlockSpec((8, 32, 128), lambda i: (i, 0, 0)),
             pl.BlockSpec((8, 32, 64), lambda i: (i, 0, 0)),

time: 220 us -> 163 us (0.74)
  Pallas kernels: 138 us -> 80.7 us
    pallas_call x1, Pallas kernels: 84.4 us -> 26.7 us  [run_spread(): pl.pallas_call(spread_factors, in_specs=[FULL, FULL], out_specs=[FULL, FU...]
where the time goes in v2:
time: 163 us; the launch traced here: 160 us
  Pallas kernels  80.7 us (50%)
  waiting for transfers between devices  37.2 us (23%)
  local copies, waits for them, and re-layouts  21.3 us (13%)
  starting transfers between devices  19.1 us (12%)
    pallas_call x1, Pallas kernels, run_attention(): pl.pallas_call(column_attention, grid=(count_res,), in_specs=[pl.BlockSpe...  34.6 us
    pallas_call x1, Pallas kernels, run_spread(): pl.pallas_call(spread_factors, in_specs=[FULL, FULL], out_specs=[FULL, FU...  26.7 us
    ppermute x2, waiting for transfers between devices, shards(): mirrors.append(lax.ppermute(half, ('row', 'col'), pairs))  21.4 us
    pallas_call x1, Pallas kernels, run_pair(): pl.pallas_call(pair_tile, grid=(8,), in_specs=[pl.BlockSpec(memory_space=...  19.4 us
    unnamed x48, local copies, waits for them, and re-layouts  17.5 us
    all_to_all x1, waiting for transfers between devices, shards(): lax.all_to_all(fragments, ('row', 'col'), split_axis=2, concat_axis=0, ti...  15.8 us
    all_to_all x1, starting transfers between devices, shards(): lax.all_to_all(fragments, ('row', 'col'), split_axis=2, concat_axis=0, ti...  10.8 us
    ppermute x2, starting transfers between devices, shards(): mirrors.append(lax.ppermute(half, ('row', 'col'), pairs))  8.34 us
  transfers between devices with their start and end apart: 3, of which 3 were waited for; matrix products, arithmetic and copies ran while one was open for 2% of the time, Pallas kernels for 0%

profile of v2, /device:TPU:7, one launch (start us, length us, event | category | flops | bytes accessed | tf_op | source)
XLA Modules:
  0.0 160.3 jit_solution(9052495961890911902)
XLA Ops:
  0.6 0.0 copy-start.19
  0.6 0.0 copy-start.20
  0.7 0.0 copy-start.22
  0.7 0.0 copy-start.18
  0.7 0.0 copy-start.17
  0.7 0.0 copy-start.21
  0.7 3.0 %copy.33 = bf16[4,512,256]{2,0,1:T(4,128)(2,1)} copy(bf16[4,512,256]{2,1,0:T(8,128)(2,1)} %param.18) | data formatting | bytes 2097152 | tf_op args[0]
  3.7 10.8 %all-to-all-start = ((bf16[1,4,128,4,256]{4,1,3,0,2:T(4,128)(2,1)}), bf16[1,4,128,4,256]{4,1,3,0,2:T(4,128)(2,1)S(1)}, u32[]{:S(2)}, u32[]{:S(2)}) async-start(bf16[1,4,128,4,256]{4,1,3,0,2:T(4,128)(2,1)} %bitcast), calls=%async_computation | async-start | bytes 2097152 | tf_op jit(solution)/shard_map/all_to_all | solution.py:398
  14.5 0.0 copy-done.19
  14.5 0.1 copy.36
  14.7 0.1 copy.35
  14.8 0.0 copy-done.22
  14.8 0.6 pad.9.offset_ref
  15.5 0.1 copy.37
  15.6 0.7 copy.38.bins_ref
  16.3 0.1 pad_add_fusion.pos_ref
  16.4 0.0 copy-start.2
  16.4 0.0 copy-start.3
  16.4 15.8 %all-to-all-done = bf16[1,4,128,4,256]{4,1,3,0,2:T(4,128)(2,1)S(1)} async-done(((bf16[1,4,128,4,256]{4,1,3,0,2:T(4,128)(2,1)}), bf16[1,4,128,4,256]{4,1,3,0,2:T(4,128)(2,1)S(1)}, u32[]{:S(2)}, u32[]{:S(2)}) %all-to-all-start) | async-done | bytes 1048608 | tf_op jit(solution)/shard_map/all_to_all | solution.py:398
  32.2 0.4 copy.34
  32.5 0.3 reshape.31
  32.8 0.0 copy-start.8
  32.9 0.9 copy-done.8
  33.8 0.9 copy-done.9
  34.7 0.9 copy-done.10
  35.6 0.9 copy-done.11
  36.5 0.9 copy-done.12
  37.4 0.8 copy-done.15
  38.2 0.8 copy-done.16
  39.1 34.6 %column_attention.1 = (bf16[512,1024]{1,0:T(8,128)(2,1)S(1)}, bf16[528,128]{1,0:T(8,128)(2,1)S(1)}, bf16[144,512]{1,0:T(8,128)(2,1)S(1)}) custom-call(bf16[4,512,256]{2,1,0:T(8,128)(2,1)S(1)} %bitcast.19, bf16[16,256]{1,0:T(8,128)(2,1)S(1)} %pad.8.feat_ref, bf16[256,256]{1,0:T(8,128)(2,1)S(1)} %copy-done.8, bf16[256,256]{1,0:T(8,128)(2,1)S(1)} %copy-done.9, ...), custom_call_target="tpu_custom_call" | custom-call | tf_op jit(solution)/shard_map/column_attention/pallas_call | solution.py:113
  73.6 0.0 copy-start.4
  73.6 0.7 copy-done.4
  74.3 0.7 copy-done.5
  74.9 26.7 %spread_factors.1 = (bf16[16,528,128]{2,1,0:T(8,128)(2,1)}, bf16[8,144,512]{2,1,0:T(8,128)(2,1)}) custom-call(bf16[528,128]{1,0:T(8,128)(2,1)} %copy-done.5, bf16[144,512]{1,0:T(8,128)(2,1)} %copy-done.4), custom_call_target="tpu_custom_call" | custom-call | tf_op jit(solution)/shard_map/spread_factors/pallas_call | solution.py:252
  101.7 1.6 copy-done
  103.3 1.3 copy-done.1
  104.6 0.8 copy-done.6
  105.3 0.8 copy-done.7
  106.1 0.9 copy-done.13
  107.0 0.9 copy-done.14
  107.9 19.4 %pair_tile.1 = (bf16[64,32,128]{2,1,0:T(8,128)(2,1)}, f32[64,32,64]{2,1,0:T(8,128)S(1)}) custom-call(s32[2]{0:T(128)S(1)} %pad_add_fusion.pos_ref, bf16[16,528,128]{2,1,0:T(8,128)(2,1)S(1)} %copy-done, bf16[8,144,512]{2,1,0:T(8,128)(2,1)S(1)} %copy-done.1, bf16[128,128]{1,0:T(8,128)(2,1)S(1)} %copy-done.6, bf16[1024,128]{1,0:T(8,128)(2,1)S(1)} %bitcast.20, ...), custom_call_target="tpu_custom_call" | custom-call | tf_op jit(solution)/shard_map/pair_tile/pallas_call | solution.py:343
  127.3 0.6 copy.41
  128.0 6.8 %collective-permute-start = (bf16[32,32,64]{2,0,1:T(8,128)(2,1)S(1)}, bf16[32,32,64]{2,0,1:T(8,128)(2,1)S(1)}, u32[]{:S(2)}, u32[]{:S(2)}) collective-permute-start(bf16[32,32,64]{2,0,1:T(8,128)(2,1)S(1)} %get-tuple-element.19), channel_id=1, source_target_pairs={{0,0},{1,1},{2,16},{3,17},{4,32},{5,33},{6,48},{7,49},{8,64},{9,65... | collective-permute-start | bytes 393224 | tf_op jit(solution)/shard_map/ppermute | solution.py:449
  134.8 1.6 collective-permute-start.1
  136.3 1.6 reshape.32
  137.9 15.8 %collective-permute-done = bf16[32,32,64]{2,0,1:T(8,128)(2,1)S(1)} collective-permute-done((bf16[32,32,64]{2,0,1:T(8,128)(2,1)S(1)}, bf16[32,32,64]{2,0,1:T(8,128)(2,1)S(1)}, u32[]{:S(2)}, u32[]{:S(2)}) %collective-permute-start) | collective-permute-done | bytes 131104 | tf_op jit(solution)/shard_map/ppermute | solution.py:449
  153.7 5.6 %collective-permute-done.1 = bf16[32,32,64]{2,0,1:T(8,128)(2,1)S(1)} collective-permute-done((bf16[32,32,64]{2,0,1:T(8,128)(2,1)S(1)}, bf16[32,32,64]{2,0,1:T(8,128)(2,1)S(1)}, u32[]{:S(2)}, u32[]{:S(2)}) %collective-permute-start.1) | collective-permute-done | bytes 131104 | tf_op jit(solution)/shard_map/ppermute | solution.py:449
  159.4 1.0 fusion
  (25 shorter events, 0.2 us)
Async XLA Ops:
  0.6 13.9 %copy-start.19 = (bf16[256,32]{0,1:T(8,128)(2,1)S(1)}, bf16[256,32]{0,1:T(8,128)(2,1)}, u32[]{:S(2)}) copy-start(bf16[256,32]{0,1:T(8,128)(2,1)} %param.28) | copy-start | bytes 49156
  0.6 14.0 %copy-start.20 = (bf16[256,32]{0,1:T(8,128)(2,1)S(1)}, bf16[256,32]{0,1:T(8,128)(2,1)}, u32[]{:S(2)}) copy-start(bf16[256,32]{0,1:T(8,128)(2,1)} %param.27) | copy-start | bytes 49156
  0.7 14.2 %copy-start.22 = (bf16[4,256]{1,0:T(4,128)(2,1)S(1)}, bf16[4,256]{1,0:T(4,128)(2,1)}, u32[]{:S(2)}) copy-start(bf16[4,256]{1,0:T(4,128)(2,1)} %param.19) | copy-start | bytes 6148
  0.7 14.2 %copy-start.18 = (bf16[65,128]{1,0:T(8,128)(2,1)S(1)}, bf16[65,128]{1,0:T(8,128)(2,1)}, u32[]{:S(2)}) copy-start(bf16[65,128]{1,0:T(8,128)(2,1)} %param.32) | copy-start | bytes 49924
  0.7 14.8 %copy-start.17 = (bf16[1024,128]{1,0:T(8,128)(2,1)S(1)}, bf16[1024,128]{1,0:T(8,128)(2,1)}, u32[]{:S(2)}) copy-start(bf16[1024,128]{1,0:T(8,128)(2,1)} %param.29) | copy-start | bytes 786436
  0.7 14.9 %copy-start.21 = (bf16[128,64]{0,1:T(8,128)(2,1)S(1)}, bf16[128,64]{0,1:T(8,128)(2,1)}, u32[]{:S(2)}) copy-start(bf16[128,64]{0,1:T(8,128)(2,1)} %param.35) | copy-start | bytes 49156
  3.7 28.4 %all-to-all-start = ((bf16[1,4,128,4,256]{4,1,3,0,2:T(4,128)(2,1)}), bf16[1,4,128,4,256]{4,1,3,0,2:T(4,128)(2,1)S(1)}, u32[]{:S(2)}, u32[]{:S(2)}) async-start(bf16[1,4,128,4,256]{4,1,3,0,2:T(4,128)(2,1)} %bitcast), calls=%async_computation | async-start | bytes 2097152 | tf_op jit(solution)/shard_map/all_to_all | solution.py:398
  16.4 16.4 %copy-start.2 = (bf16[256,1024]{1,0:T(8,128)(2,1)S(1)}, bf16[256,1024]{1,0:T(8,128)(2,1)}, u32[]{:S(2)}) copy-start(bf16[256,1024]{1,0:T(8,128)(2,1)} %we_ref.1) | copy-start | bytes 1572868
  16.4 16.4 %copy-start.3 = (bf16[1024,256]{1,0:T(8,128)(2,1)S(1)}, bf16[1024,256]{1,0:T(8,128)(2,1)}, u32[]{:S(2)}) copy-start(bf16[1024,256]{1,0:T(8,128)(2,1)} %ws_ref.1) | copy-start | bytes 1572868
  32.8 0.9 copy-start.8
  33.8 0.9 copy-start.9
  34.7 0.9 copy-start.10
  35.6 0.9 copy-start.11
  36.5 0.9 copy-start.12
  37.4 0.8 copy-start.15
  38.2 0.8 copy-start.16
  73.6 0.7 copy-start.4
  74.3 0.7 copy-start.5
  101.7 1.6 %copy-start = (bf16[16,528,128]{2,1,0:T(8,128)(2,1)S(1)}, bf16[16,528,128]{2,1,0:T(8,128)(2,1)}, u32[]{:S(2)}) copy-start(bf16[16,528,128]{2,1,0:T(8,128)(2,1)} %get-tuple-element.13.a_ref) | copy-start | bytes 6488068
  103.3 1.3 copy-start.1
  104.6 0.8 copy-start.6
  105.3 0.8 copy-start.7
  106.1 0.9 copy-start.13
  107.0 0.9 copy-start.14
  128.0 25.7 %collective-permute-start = (bf16[32,32,64]{2,0,1:T(8,128)(2,1)S(1)}, bf16[32,32,64]{2,0,1:T(8,128)(2,1)S(1)}, u32[]{:S(2)}, u32[]{:S(2)}) collective-permute-start(bf16[32,32,64]{2,0,1:T(8,128)(2,1)S(1)} %get-tuple-element.19), channel_id=1, source_target_pairs={{0,0},{1,1},{2,16},{3,17},{4,32},{5,33},{6,48},{7,49},{8,64},{9,65... | collective-permute-start | bytes 393224 | tf_op jit(solution)/shard_map/ppermute | solution.py:449
  134.8 24.6 %collective-permute-start.1 = (bf16[32,32,64]{2,0,1:T(8,128)(2,1)S(1)}, bf16[32,32,64]{2,0,1:T(8,128)(2,1)S(1)}, u32[]{:S(2)}, u32[]{:S(2)}) collective-permute-start(bf16[32,32,64]{2,0,1:T(8,128)(2,1)S(1)} %get-tuple-element.20), channel_id=1, source_target_pairs={{0,1},{1,0},{2,17},{3,16},{4,33},{5,32},{6,49},{7,48},{8,65},{9,64... | collective-permute-start | bytes 393224 | tf_op jit(solution)/shard_map/ppermute | solution.py:449

commit v3 on v2

--- a/solution.py
+++ b/solution.py
@@ -11,6 +11,7 @@
 HEADS = 8
 HEAD = 32
 CLIP = 32
+VMEM_LIMIT = 67043328
 MESH = pl.DeviceIdType.MESH
 FULL = pl.BlockSpec(memory_space=pltpu.VMEM)
 
@@ -132,7 +133,7 @@
             pltpu.VMEM((seqs, width), jnp.float32),
         ],
         compiler_params=pltpu.CompilerParams(
-            dimension_semantics=("arbitrary",), vmem_limit_bytes=48 * 1024 * 1024
+            dimension_semantics=("arbitrary",), vmem_limit_bytes=VMEM_LIMIT
         ),
         name="column_attention",
     )(x, feat, *weights)
@@ -269,7 +270,6 @@
 
 
 def pair_tile(
-    pos_ref,
     a_ref,
     b_ref,
     offset_ref,
@@ -278,13 +278,55 @@
     shrink_ref,
     bins_ref,
     pair_ref,
-    logit_ref,
+    distogram_ref,
     c_scr,
     x_scr,
     right_scr,
+    own_scr,
+    out_scr,
+    in_scr,
+    turn_scr,
+    send_sem,
+    recv_sem,
 ):
     step = pl.program_id(0)
     seqs = b_ref.shape[2]
+    r, c = lax.axis_index("row"), lax.axis_index("col")
+    mirror_row, parity = c // 2, c % 2
+    diagonal = mirror_row == r
+    barrier = pltpu.get_barrier_semaphore()
+
+    def mirror_copy(number):
+        return pltpu.make_async_remote_copy(
+            src_ref=out_scr.at[number],
+            dst_ref=in_scr.at[parity, number % 4],
+            send_sem=send_sem.at[number],
+            recv_sem=recv_sem.at[parity, number % 4],
+            device_id=(mirror_row, 2 * r + number // 4),
+            device_id_type=MESH,
+        )
+
+    def stays(number):
+        return jnp.logical_and(diagonal, number // 4 == parity)
+
+    def dispatch(number):
+        @pl.when(jnp.logical_not(stays(number)))
+        def _():
+            mirror_copy(number).start()
+
+    @pl.when(step == 0)
+    def _():
+        for h in range(2):
+
+            @pl.when(jnp.logical_not(jnp.logical_and(diagonal, parity == h)))
+            def _(h=h):
+                pl.semaphore_signal(
+                    barrier, inc=1, device_id=(mirror_row, 2 * r + h), device_id_type=MESH
+                )
+
+    @pl.when(step == 1)
+    def _():
+        pl.semaphore_wait(barrier, 2 - jnp.where(diagonal, 1, 0))
 
     @pl.when(step == 0)
     def _():
@@ -295,6 +337,11 @@
     outer = mm(b_ref[:, :128, :].reshape(1024, seqs), factors)
     c_scr[0] = outer[:, :128]
     c_scr[1] = outer[:, 128:]
+
+    @pl.when(step > 0)
+    def _():
+        dispatch(step - 1)
+
     lane = lax.broadcasted_iota(jnp.int32, (32, 128), 1)
     low = lane < 64
     even = lane % 64 < 32
@@ -321,7 +368,7 @@
     projected = mm(x_scr[...], project_ref[...])
     index = lax.broadcasted_iota(jnp.int32, (256, 128), 0)
     bins = lax.broadcasted_iota(jnp.int32, (256, 128), 1)
-    offset = (pos_ref[1] + index % 32) - (pos_ref[0] + step * 8 + index // 32)
+    offset = (c * 32 + index % 32) - (r * 64 + step * 8 + index // 32)
     onehot = jnp.where(jnp.clip(offset, -CLIP, CLIP) + CLIP == bins, 1.0, 0.0)
     relative = mm(onehot.astype(jnp.bfloat16), offset_ref[...])
     left0 = a_ref[2 * step, seqs:, :].astype(jnp.float32)
@@ -335,38 +382,82 @@
     ).astype(jnp.bfloat16)
     final = (start + mm(hidden, shrink_ref[...])).astype(jnp.bfloat16)
     pair_ref[...] = final.reshape(8, 32, 128)
-    logit_ref[...] = mm(final, bins_ref[...]).reshape(8, 32, 64)
-
-
-def run_pair(pos, a_all, b_all, offset, project, expand, shrink, bins):
-    seqs = b_all.shape[2]
+    logits = mm(final, bins_ref[...])
+    own_scr[step] = logits
+    packed = jnp.where(bins[:128] < 64, logits[:128], logits[128:]).astype(jnp.bfloat16)
+    out_scr[step] = packed
+
+    @pl.when(stays(step))
+    def _():
+        in_scr[parity, step % 4] = packed
+
+    @pl.when(step == pl.num_programs(0) - 1)
+    def _():
+        dispatch(step)
+        for quarter in range(4):
+            for k in range(2):
+
+                @pl.when(jnp.logical_not(jnp.logical_and(diagonal, parity == k)))
+                def _(k=k, quarter=quarter):
+                    pltpu.make_async_remote_copy(
+                        src_ref=in_scr.at[k, quarter],
+                        dst_ref=in_scr.at[k, quarter],
+                        send_sem=recv_sem.at[k, quarter],
+                        recv_sem=recv_sem.at[k, quarter],
+                        device_id=(mirror_row, 2 * r + k),
+                        device_id_type=MESH,
+                    ).wait_recv()
+
+                for i in range(4):
+                    rows = in_scr[k, quarter, 32 * i : 32 * i + 32, :].astype(jnp.float32)
+                    first = k * 1024 + quarter * 8 + i
+                    turn_scr[pl.ds(first, 32, stride=32), :] = rows
+                    turn_scr[pl.ds(first + 4, 32, stride=32), :] = pltpu.roll(rows, 64, 1)
+        for number in range(8):
+            total = own_scr[number] + turn_scr[256 * number : 256 * number + 256, :]
+            distogram_ref[8 * number : 8 * number + 8] = (
+                total[:, :64].astype(jnp.bfloat16).reshape(8, 32, 64)
+            )
+        for number in range(8):
+
+            @pl.when(jnp.logical_not(stays(number)))
+            def _(number=number):
+                mirror_copy(number).wait_send()
+
+
+def run_pair(a_all, b_all, offset, project, expand, shrink, bins):
     return pl.pallas_call(
         pair_tile,
         grid=(8,),
-        in_specs=[
-            pl.BlockSpec(memory_space=pltpu.SMEM),
-            FULL,
-            FULL,
-        ]
+        in_specs=[FULL, FULL]
         + [resident(one.shape) for one in (offset, project, expand, shrink, bins)],
         out_specs=[
             pl.BlockSpec((8, 32, 128), lambda i: (i, 0, 0)),
-            pl.BlockSpec((8, 32, 64), lambda i: (i, 0, 0)),
+            pl.BlockSpec((64, 32, 64), lambda i: (0, 0, 0)),
         ],
         out_shape=[
             jax.ShapeDtypeStruct((64, 32, 128), jnp.bfloat16),
-            jax.ShapeDtypeStruct((64, 32, 64), jnp.float32),
+            jax.ShapeDtypeStruct((64, 32, 64), jnp.bfloat16),
         ],
         scratch_shapes=[
             pltpu.VMEM((2, 1024, 128), jnp.float32),
             pltpu.VMEM((256, 1024), jnp.bfloat16),
             pltpu.VMEM((32, 128), jnp.float32),
+            pltpu.VMEM((8, 256, 128), jnp.float32),
+            pltpu.VMEM((8, 128, 128), jnp.bfloat16),
+            pltpu.VMEM((2, 4, 128, 128), jnp.bfloat16),
+            pltpu.VMEM((2048, 128), jnp.float32),
+            pltpu.SemaphoreType.DMA((8,)),
+            pltpu.SemaphoreType.DMA((2, 4)),
         ],
         compiler_params=pltpu.CompilerParams(
-            dimension_semantics=("arbitrary",), vmem_limit_bytes=48 * 1024 * 1024
+            dimension_semantics=("arbitrary",),
+            vmem_limit_bytes=VMEM_LIMIT,
+            collective_id=1,
+            has_side_effects=True,
         ),
         name="pair_tile",
-    )(pos, a_all, b_all, offset, project, expand, shrink, bins)
+    )(a_all, b_all, offset, project, expand, shrink, bins)
 
 
 def shards(
@@ -419,39 +510,21 @@
     )
     alignment_output = updated.reshape(seqs, res_here, width)
     a_all, b_all = run_spread(a_block, b_block, rows, cols)
-    r, c = lax.axis_index("row"), lax.axis_index("col")
     factor = former_factor_matrix.shape[1]
     project = (
         factor_mean_projection.reshape(factor, factor, -1)
         .transpose(1, 0, 2)
         .reshape(factor * factor, -1)
     )
-    row_len, col_len = residues // rows, residues // cols
-    pos = jnp.stack([r * row_len, c * col_len]).astype(jnp.int32)
-    pair_output, logits = run_pair(
-        pos,
+    pair_output, distogram = run_pair(
         a_all,
         b_all,
         jnp.pad(offset_embedding_matrix, ((0, 127 - 2 * CLIP), (0, 0))),
         project,
         grid_transition_expand,
         grid_transition_shrink,
-        distance_bins_matrix,
+        jnp.concatenate([distance_bins_matrix] * 2, axis=1),
     )
-    rounded = logits.astype(jnp.bfloat16)
-    mirrors = []
-    for k in range(2):
-        pairs = []
-        for rr in range(rows):
-            for cc in range(cols):
-                pairs.append((rr * cols + cc, cc // 2 * cols + 2 * rr + (cc % 2 ^ k)))
-        half = lax.dynamic_slice_in_dim(rounded, (c % 2 ^ k) * col_len, col_len, 0)
-        mirrors.append(lax.ppermute(half, ("row", "col"), pairs))
-    flip = c % 2 == 0
-    first = jnp.where(flip, mirrors[0], mirrors[1])
-    second = jnp.where(flip, mirrors[1], mirrors[0])
-    mirror = jnp.concatenate([first, second], axis=1)
-    distogram = (logits + mirror.transpose(1, 0, 2).astype(jnp.float32)).astype(jnp.bfloat16)
     return (alignment_output, pair_output, distogram)
 
 

time: 163 us -> 137 us (0.84); the launches traced: 160 us -> 136 us
  waiting for transfers between devices: 37.2 us -> 13.8 us
  Pallas kernels: 80.7 us -> 96.4 us
  starting transfers between devices: 19.1 us -> 10.8 us
  local copies, waits for them, and re-layouts: 21.3 us -> 13.3 us
    ppermute x2 -> x0, waiting for transfers between devices: 21.4 us -> none  [shards(): mirrors.append(lax.ppermute(half, ('row', 'col'), pairs))]
    pallas_call x1, Pallas kernels: 19.4 us -> 32.7 us  [run_pair(): pl.pallas_call(pair_tile, grid=(8,), in_specs=[FULL, FULL] + [resident(on...]
    unnamed x48 -> x16, local copies, waits for them, and re-layouts: 17.5 us -> 6.92 us
    ppermute x2 -> x0, starting transfers between devices: 8.34 us -> none  [shards(): mirrors.append(lax.ppermute(half, ('row', 'col'), pairs))]
    pallas_call x1, Pallas kernels: 34.6 us -> 37 us  [run_attention(): pl.pallas_call(column_attention, grid=(count_res,), in_specs=[pl.BlockSpe...]
    all_to_all x1, waiting for transfers between devices: 15.8 us -> 13.8 us  [shards(): lax.all_to_all(fragments, ('row', 'col'), split_axis=2, concat_axis=0, ti...]
  transfers between devices with their start and end apart: 3 -> 1, of which waited for: 3 -> 1; matrix products, arithmetic and copies ran while one was open for 2% -> 3% of each run, Pallas kernels for 0% -> 0%
where the time goes in v3:
time: 137 us; the launch traced here: 136 us
  Pallas kernels  96.4 us (70%)
  waiting for transfers between devices  13.8 us (10%)
  local copies, waits for them, and re-layouts  13.3 us (10%)
  starting transfers between devices  10.8 us (8%)
  other arithmetic  1.37 us (1%)
    pallas_call x1, Pallas kernels, run_attention(): pl.pallas_call(column_attention, grid=(count_res,), in_specs=[pl.BlockSpe...  37 us
    pallas_call x1, Pallas kernels, run_pair(): pl.pallas_call(pair_tile, grid=(8,), in_specs=[FULL, FULL] + [resident(on...  32.7 us
    pallas_call x1, Pallas kernels, run_spread(): pl.pallas_call(spread_factors, in_specs=[FULL, FULL], out_specs=[FULL, FU...  26.7 us
    all_to_all x1, waiting for transfers between devices, shards(): lax.all_to_all(fragments, ('row', 'col'), split_axis=2, concat_axis=0, ti...  13.8 us
    all_to_all x1, starting transfers between devices, shards(): lax.all_to_all(fragments, ('row', 'col'), split_axis=2, concat_axis=0, ti...  10.8 us
    unnamed x16, local copies, waits for them, and re-layouts  6.92 us
  transfers between devices with their start and end apart: 1, of which 1 were waited for; matrix products, arithmetic and copies ran while one was open for 3% of the time, Pallas kernels for 0%

profile of v3, /device:TPU:7, one launch (start us, length us, event | category | flops | bytes accessed | tf_op | source)
XLA Modules:
  0.0 136.4 jit_solution(17000231316695589074)
XLA Ops:
  0.6 0.0 copy-start.5
  0.6 0.0 copy-start.1
  0.7 0.0 copy-start.2
  0.7 0.0 copy-start.3
  0.7 0.0 copy-start.4
  0.7 0.0 copy-start
  0.7 3.0 %copy.33 = bf16[4,512,256]{2,0,1:T(4,128)(2,1)} copy(bf16[4,512,256]{2,1,0:T(8,128)(2,1)} %param.18) | data formatting | bytes 2097152 | tf_op args[0]
  3.7 10.8 %all-to-all-start = ((bf16[1,4,128,4,256]{4,1,3,0,2:T(4,128)(2,1)}), bf16[1,4,128,4,256]{4,1,3,0,2:T(4,128)(2,1)S(1)}, u32[]{:S(2)}, u32[]{:S(2)}) async-start(bf16[1,4,128,4,256]{4,1,3,0,2:T(4,128)(2,1)} %bitcast), calls=%async_computation | async-start | bytes 2097152 | tf_op jit(solution)/shard_map/all_to_all | solution.py:489
  14.5 0.0 copy-done.5
  14.5 0.6 pad.8.feat_ref
  15.1 0.0 copy-done.1
  15.1 0.6 pad.9.offset_ref
  15.7 0.0 copy-done.2
  15.7 0.1 copy.38
  15.9 0.0 copy-done.3
  15.9 0.1 copy.35
  16.0 0.0 copy-done.4
  16.0 0.1 copy.36
  16.1 0.0 copy-done
  16.1 0.8 copy.37
  17.0 0.7 pad_maximum_fusion.1.bins_ref
  17.7 0.7 pad_maximum_fusion.factor_ref
  18.3 13.8 %all-to-all-done = bf16[1,4,128,4,256]{4,1,3,0,2:T(4,128)(2,1)S(1)} async-done(((bf16[1,4,128,4,256]{4,1,3,0,2:T(4,128)(2,1)}), bf16[1,4,128,4,256]{4,1,3,0,2:T(4,128)(2,1)S(1)}, u32[]{:S(2)}, u32[]{:S(2)}) %all-to-all-start) | async-done | bytes 1048608 | tf_op jit(solution)/shard_map/all_to_all | solution.py:489
  32.2 0.4 copy.34
  32.5 1.1 reshape.31
  33.6 37.0 %column_attention.1 = (bf16[512,1024]{1,0:T(8,128)(2,1)}, bf16[528,128]{1,0:T(8,128)(2,1)}, bf16[144,512]{1,0:T(8,128)(2,1)}) custom-call(bf16[4,512,256]{2,1,0:T(8,128)(2,1)} %bitcast.13, bf16[16,256]{1,0:T(8,128)(2,1)} %pad.8.feat_ref, bf16[256,256]{1,0:T(8,128)(2,1)} %wq_ref.1, bf16[256,256]{1,0:T(8,128)(2,1)} %wk_ref.1, bf16[256,256]{1,0:T(8,128)(2,1)} %wv_ref.1, ...), custom_call_target="tpu_custom_call" | custom-call | tf_op jit(solution)/shard_map/column_attention/pallas_call | solution.py:114
  70.6 2.6 %reshape.32 = bf16[512,4,256]{2,1,0:T(4,128)(2,1)} reshape(bf16[512,1024]{1,0:T(8,128)(2,1)} %get-tuple-element.10) | data formatting | bytes 2097152 | tf_op jit(solution)/shard_map/reshape | solution.py:511
  73.2 26.7 %spread_factors.1 = (bf16[16,528,128]{2,1,0:T(8,128)(2,1)}, bf16[8,144,512]{2,1,0:T(8,128)(2,1)}) custom-call(bf16[528,128]{1,0:T(8,128)(2,1)} %get-tuple-element.11.a_ref, bf16[144,512]{1,0:T(8,128)(2,1)} %get-tuple-element.12.b_ref), custom_call_target="tpu_custom_call" | custom-call | tf_op jit(solution)/shard_map/spread_factors/pallas_call | solution.py:253
  100.0 32.7 %pair_tile.1 = (bf16[64,32,128]{2,1,0:T(8,128)(2,1)}, bf16[64,32,64]{2,1,0:T(8,128)(2,1)}) custom-call(bf16[16,528,128]{2,1,0:T(8,128)(2,1)} %get-tuple-element.13.a_ref, bf16[8,144,512]{2,1,0:T(8,128)(2,1)} %get-tuple-element.14.b_ref, bf16[128,128]{1,0:T(8,128)(2,1)} %pad.9.offset_ref, bf16[1024,128]{1,0:T(8,128)(2,1)} %bitcast.15, ...), custom_call_target="tpu_custom_call" | custom-call | tf_op jit(solution)/shard_map/pair_tile/pallas_call | solution.py:429
  132.7 1.9 %copy.42 = bf16[64,32,128]{2,1,0:T(8,128)(2,1)} copy(bf16[64,32,128]{2,1,0:T(8,128)(2,1)} %get-tuple-element.21) | data formatting | bytes 1048576
  134.5 1.9 %copy.43 = bf16[64,32,64]{2,1,0:T(8,128)(2,1)} copy(bf16[64,32,64]{2,1,0:T(8,128)(2,1)} %get-tuple-element.22) | data formatting | bytes 524288
  (2 shorter events, 0.0 us)
Async XLA Ops:
  0.6 13.9 %copy-start.5 = (bf16[4,256]{1,0:T(4,128)(2,1)S(1)}, bf16[4,256]{1,0:T(4,128)(2,1)}, u32[]{:S(2)}) copy-start(bf16[4,256]{1,0:T(4,128)(2,1)} %param.19) | copy-start | bytes 6148
  0.6 14.5 %copy-start.1 = (bf16[65,128]{1,0:T(8,128)(2,1)S(1)}, bf16[65,128]{1,0:T(8,128)(2,1)}, u32[]{:S(2)}) copy-start(bf16[65,128]{1,0:T(8,128)(2,1)} %param.32) | copy-start | bytes 49924
  0.7 15.1 %copy-start.2 = (bf16[128,64]{0,1:T(8,128)(2,1)S(1)}, bf16[128,64]{0,1:T(8,128)(2,1)}, u32[]{:S(2)}) copy-start(bf16[128,64]{0,1:T(8,128)(2,1)} %param.35) | copy-start | bytes 49156
  0.7 15.2 %copy-start.3 = (bf16[256,32]{0,1:T(8,128)(2,1)S(1)}, bf16[256,32]{0,1:T(8,128)(2,1)}, u32[]{:S(2)}) copy-start(bf16[256,32]{0,1:T(8,128)(2,1)} %param.27) | copy-start | bytes 49156
  0.7 15.3 %copy-start.4 = (bf16[256,32]{0,1:T(8,128)(2,1)S(1)}, bf16[256,32]{0,1:T(8,128)(2,1)}, u32[]{:S(2)}) copy-start(bf16[256,32]{0,1:T(8,128)(2,1)} %param.28) | copy-start | bytes 49156
  0.7 15.5 %copy-start = (bf16[1024,128]{1,0:T(8,128)(2,1)S(1)}, bf16[1024,128]{1,0:T(8,128)(2,1)}, u32[]{:S(2)}) copy-start(bf16[1024,128]{1,0:T(8,128)(2,1)} %param.29) | copy-start | bytes 786436
  3.7 28.4 %all-to-all-start = ((bf16[1,4,128,4,256]{4,1,3,0,2:T(4,128)(2,1)}), bf16[1,4,128,4,256]{4,1,3,0,2:T(4,128)(2,1)S(1)}, u32[]{:S(2)}, u32[]{:S(2)}) async-start(bf16[1,4,128,4,256]{4,1,3,0,2:T(4,128)(2,1)} %bitcast), calls=%async_computation | async-start | bytes 2097152 | tf_op jit(solution)/shard_map/all_to_all | solution.py:489

commit v4 on v3

--- a/solution.py
+++ b/solution.py
@@ -63,23 +63,27 @@
     ones = jnp.ones((seqs, 128), jnp.bfloat16)
     v_scr[0] = jnp.concatenate([v[:, :128], ones], axis=1)
     v_scr[1] = jnp.concatenate([v[:, 128:], ones], axis=1)
-    acc_scr[...] = jnp.zeros_like(acc_scr)
     lane = lax.broadcasted_iota(jnp.int32, (seqs, 256), 1)
     factor = math.log2(math.e) / math.sqrt(HEAD)
 
-    def one_head(h, carry):
-        group = h // 4
-        q = jnp.where(lane // HEAD == h, q_scr[...], jnp.zeros((), jnp.bfloat16))
-        scores = mm(q, kt_scr[...])
-        top = jnp.max(scores, axis=-1, keepdims=True)
-        weights = jnp.exp2((scores - top) * factor).astype(jnp.bfloat16)
-        values = jnp.where(
-            lane % 128 // HEAD == h % 4, v_scr[group], jnp.zeros((), jnp.bfloat16)
-        )
-        acc_scr[group] += mm(weights, values)
+    def one_group(group, carry):
+        total = None
+        for k in range(HEADS // 2):
+            q = jnp.where(
+                lane // HEAD == group * 4 + k, q_scr[...], jnp.zeros((), jnp.bfloat16)
+            )
+            scores = mm(q, kt_scr[...])
+            top = jnp.max(scores, axis=-1, keepdims=True)
+            weights = jnp.exp2((scores - top) * factor).astype(jnp.bfloat16)
+            values = jnp.where(
+                lane % 128 // HEAD == k, v_scr[group], jnp.zeros((), jnp.bfloat16)
+            )
+            part = mm(weights, values)
+            total = part if total is None else total + part
+        acc_scr[group] = total
         return carry
 
-    lax.fori_loop(0, HEADS, one_head, 0)
+    lax.fori_loop(0, 2, one_group, 0)
     attended = jnp.concatenate(
         [
             acc_scr[0, :, :128] / acc_scr[0, :, 128:],

time: 137 us -> 127 us (0.927)
  Pallas kernels: 96.4 us -> 86.8 us
    pallas_call x1, Pallas kernels: 37 us -> 27.5 us  [run_attention(): pl.pallas_call(column_attention, grid=(count_res,), in_specs=[pl.BlockSpe...]
where the time goes in v4:
time: 127 us
  Pallas kernels  86.8 us (68%)
  waiting for transfers between devices  13.8 us (11%)
  local copies, waits for them, and re-layouts  13.3 us (10%)
  starting transfers between devices  10.8 us (9%)
  other arithmetic  1.37 us (1%)
    pallas_call x1, Pallas kernels, run_pair(): pl.pallas_call(pair_tile, grid=(8,), in_specs=[FULL, FULL] + [resident(on...  32.6 us
    pallas_call x1, Pallas kernels, run_attention(): pl.pallas_call(column_attention, grid=(count_res,), in_specs=[pl.BlockSpe...  27.5 us
    pallas_call x1, Pallas kernels, run_spread(): pl.pallas_call(spread_factors, in_specs=[FULL, FULL], out_specs=[FULL, FU...  26.7 us
    all_to_all x1, waiting for transfers between devices, shards(): lax.all_to_all(fragments, ('row', 'col'), split_axis=2, concat_axis=0, ti...  13.8 us
    all_to_all x1, starting transfers between devices, shards(): lax.all_to_all(fragments, ('row', 'col'), split_axis=2, concat_axis=0, ti...  10.8 us
    unnamed x16, local copies, waits for them, and re-layouts  6.92 us
    reshape x1, local copies, waits for them, and re-layouts, shards(): alignment_output = updated.reshape(seqs, res_here, width)  2.63 us
  transfers between devices with their start and end apart: 1, of which 1 were waited for; matrix products, arithmetic and copies ran while one was open for 3% of the time, Pallas kernels for 0%

profile of v4, /device:TPU:7, one launch (start us, length us, event | category | flops | bytes accessed | tf_op | source)
XLA Modules:
  0.0 126.8 jit_solution(4494498265309136920)
XLA Ops:
  0.6 0.0 copy-start.5
  0.6 0.0 copy-start.1
  0.7 0.0 copy-start.2
  0.7 0.0 copy-start.3
  0.7 0.0 copy-start.4
  0.7 0.0 copy-start
  0.7 3.0 %copy.33 = bf16[4,512,256]{2,0,1:T(4,128)(2,1)} copy(bf16[4,512,256]{2,1,0:T(8,128)(2,1)} %param.18) | data formatting | bytes 2097152 | tf_op args[0]
  3.7 10.8 %all-to-all-start = ((bf16[1,4,128,4,256]{4,1,3,0,2:T(4,128)(2,1)}), bf16[1,4,128,4,256]{4,1,3,0,2:T(4,128)(2,1)S(1)}, u32[]{:S(2)}, u32[]{:S(2)}) async-start(bf16[1,4,128,4,256]{4,1,3,0,2:T(4,128)(2,1)} %bitcast), calls=%async_computation | async-start | bytes 2097152 | tf_op jit(solution)/shard_map/all_to_all | solution.py:493
  14.5 0.0 copy-done.5
  14.5 0.6 pad.8.feat_ref
  15.1 0.0 copy-done.1
  15.1 0.6 pad.9.offset_ref
  15.7 0.0 copy-done.2
  15.7 0.1 copy.38
  15.9 0.0 copy-done.3
  15.9 0.1 copy.35
  16.0 0.0 copy-done.4
  16.0 0.1 copy.36
  16.1 0.0 copy-done
  16.1 0.8 copy.37
  17.0 0.7 pad_maximum_fusion.1.bins_ref
  17.7 0.7 pad_maximum_fusion.factor_ref
  18.3 13.8 %all-to-all-done = bf16[1,4,128,4,256]{4,1,3,0,2:T(4,128)(2,1)S(1)} async-done(((bf16[1,4,128,4,256]{4,1,3,0,2:T(4,128)(2,1)}), bf16[1,4,128,4,256]{4,1,3,0,2:T(4,128)(2,1)S(1)}, u32[]{:S(2)}, u32[]{:S(2)}) %all-to-all-start) | async-done | bytes 1048608 | tf_op jit(solution)/shard_map/all_to_all | solution.py:493
  32.2 0.4 copy.34
  32.5 1.1 reshape.31
  33.6 27.5 %column_attention.1 = (bf16[512,1024]{1,0:T(8,128)(2,1)}, bf16[528,128]{1,0:T(8,128)(2,1)}, bf16[144,512]{1,0:T(8,128)(2,1)}) custom-call(bf16[4,512,256]{2,1,0:T(8,128)(2,1)} %bitcast.13, bf16[16,256]{1,0:T(8,128)(2,1)} %pad.8.feat_ref, bf16[256,256]{1,0:T(8,128)(2,1)} %wq_ref.1, bf16[256,256]{1,0:T(8,128)(2,1)} %wk_ref.1, bf16[256,256]{1,0:T(8,128)(2,1)} %wv_ref.1, ...), custom_call_target="tpu_custom_call" | custom-call | tf_op jit(solution)/shard_map/column_attention/pallas_call | solution.py:118
  61.1 2.6 %reshape.32 = bf16[512,4,256]{2,1,0:T(4,128)(2,1)} reshape(bf16[512,1024]{1,0:T(8,128)(2,1)} %get-tuple-element.10) | data formatting | bytes 2097152 | tf_op jit(solution)/shard_map/reshape | solution.py:515
  63.8 26.7 %spread_factors.1 = (bf16[16,528,128]{2,1,0:T(8,128)(2,1)}, bf16[8,144,512]{2,1,0:T(8,128)(2,1)}) custom-call(bf16[528,128]{1,0:T(8,128)(2,1)} %get-tuple-element.11.a_ref, bf16[144,512]{1,0:T(8,128)(2,1)} %get-tuple-element.12.b_ref), custom_call_target="tpu_custom_call" | custom-call | tf_op jit(solution)/shard_map/spread_factors/pallas_call | solution.py:257
  90.5 32.6 %pair_tile.1 = (bf16[64,32,128]{2,1,0:T(8,128)(2,1)}, bf16[64,32,64]{2,1,0:T(8,128)(2,1)}) custom-call(bf16[16,528,128]{2,1,0:T(8,128)(2,1)} %get-tuple-element.13.a_ref, bf16[8,144,512]{2,1,0:T(8,128)(2,1)} %get-tuple-element.14.b_ref, bf16[128,128]{1,0:T(8,128)(2,1)} %pad.9.offset_ref, bf16[1024,128]{1,0:T(8,128)(2,1)} %bitcast.15, ...), custom_call_target="tpu_custom_call" | custom-call | tf_op jit(solution)/shard_map/pair_tile/pallas_call | solution.py:433
  123.1 1.9 %copy.42 = bf16[64,32,128]{2,1,0:T(8,128)(2,1)} copy(bf16[64,32,128]{2,1,0:T(8,128)(2,1)} %get-tuple-element.21) | data formatting | bytes 1048576
  125.0 1.9 %copy.43 = bf16[64,32,64]{2,1,0:T(8,128)(2,1)} copy(bf16[64,32,64]{2,1,0:T(8,128)(2,1)} %get-tuple-element.22) | data formatting | bytes 524288
  (2 shorter events, 0.0 us)
Async XLA Ops:
  0.6 13.9 %copy-start.5 = (bf16[4,256]{1,0:T(4,128)(2,1)S(1)}, bf16[4,256]{1,0:T(4,128)(2,1)}, u32[]{:S(2)}) copy-start(bf16[4,256]{1,0:T(4,128)(2,1)} %param.19) | copy-start | bytes 6148
  0.6 14.5 %copy-start.1 = (bf16[65,128]{1,0:T(8,128)(2,1)S(1)}, bf16[65,128]{1,0:T(8,128)(2,1)}, u32[]{:S(2)}) copy-start(bf16[65,128]{1,0:T(8,128)(2,1)} %param.32) | copy-start | bytes 49924
  0.7 15.1 %copy-start.2 = (bf16[128,64]{0,1:T(8,128)(2,1)S(1)}, bf16[128,64]{0,1:T(8,128)(2,1)}, u32[]{:S(2)}) copy-start(bf16[128,64]{0,1:T(8,128)(2,1)} %param.35) | copy-start | bytes 49156
  0.7 15.2 %copy-start.3 = (bf16[256,32]{0,1:T(8,128)(2,1)S(1)}, bf16[256,32]{0,1:T(8,128)(2,1)}, u32[]{:S(2)}) copy-start(bf16[256,32]{0,1:T(8,128)(2,1)} %param.27) | copy-start | bytes 49156
  0.7 15.3 %copy-start.4 = (bf16[256,32]{0,1:T(8,128)(2,1)S(1)}, bf16[256,32]{0,1:T(8,128)(2,1)}, u32[]{:S(2)}) copy-start(bf16[256,32]{0,1:T(8,128)(2,1)} %param.28) | copy-start | bytes 49156
  0.7 15.5 %copy-start = (bf16[1024,128]{1,0:T(8,128)(2,1)S(1)}, bf16[1024,128]{1,0:T(8,128)(2,1)}, u32[]{:S(2)}) copy-start(bf16[1024,128]{1,0:T(8,128)(2,1)} %param.29) | copy-start | bytes 786436
  3.7 28.4 %all-to-all-start = ((bf16[1,4,128,4,256]{4,1,3,0,2:T(4,128)(2,1)}), bf16[1,4,128,4,256]{4,1,3,0,2:T(4,128)(2,1)S(1)}, u32[]{:S(2)}, u32[]{:S(2)}) async-start(bf16[1,4,128,4,256]{4,1,3,0,2:T(4,128)(2,1)} %bitcast), calls=%async_computation | async-start | bytes 2097152 | tf_op jit(solution)/shard_map/all_to_all | solution.py:493

commit v5 on v4

--- a/solution.py
+++ b/solution.py
@@ -303,15 +303,15 @@
     def mirror_copy(number):
         return pltpu.make_async_remote_copy(
             src_ref=out_scr.at[number],
-            dst_ref=in_scr.at[parity, number % 4],
+            dst_ref=in_scr.at[parity, number % 2],
             send_sem=send_sem.at[number],
-            recv_sem=recv_sem.at[parity, number % 4],
-            device_id=(mirror_row, 2 * r + number // 4),
+            recv_sem=recv_sem.at[parity, number % 2],
+            device_id=(mirror_row, 2 * r + number // 2),
             device_id_type=MESH,
         )
 
     def stays(number):
-        return jnp.logical_and(diagonal, number // 4 == parity)
+        return jnp.logical_and(diagonal, number // 2 == parity)
 
     def dispatch(number):
         @pl.when(jnp.logical_not(stays(number)))
@@ -337,47 +337,30 @@
         for d in range(8):
             right_scr[4 * d : 4 * d + 4, :] = b_ref[d, 128:, :128].astype(jnp.float32)[:4]
 
-    factors = jnp.concatenate([a_ref[2 * step, :seqs, :], a_ref[2 * step + 1, :seqs, :]], axis=1)
+    factors = jnp.concatenate([a_ref[4 * step + n, :seqs, :] for n in range(4)], axis=1)
     outer = mm(b_ref[:, :128, :].reshape(1024, seqs), factors)
-    c_scr[0] = outer[:, :128]
-    c_scr[1] = outer[:, 128:]
+    for part in range(4):
+        c_scr[part] = outer[:, 128 * part : 128 * part + 128]
 
     @pl.when(step > 0)
     def _():
         dispatch(step - 1)
 
-    lane = lax.broadcasted_iota(jnp.int32, (32, 128), 1)
-    low = lane < 64
-    even = lane % 64 < 32
-    for part in range(2):
-        for e in range(0, 32, 4):
-            y = [c_scr[part, pl.ds(e + k, 32, stride=32), :] for k in range(4)]
-            u = [
-                jnp.where(low, y[0], pltpu.roll(y[2], 64, 1)),
-                jnp.where(low, y[1], pltpu.roll(y[3], 64, 1)),
-                jnp.where(low, pltpu.roll(y[0], 64, 1), y[2]),
-                jnp.where(low, pltpu.roll(y[1], 64, 1), y[3]),
-            ]
-            z = [
-                jnp.where(even, u[0], pltpu.roll(u[1], 32, 1)),
-                jnp.where(even, pltpu.roll(u[0], 96, 1), u[1]),
-                jnp.where(even, u[2], pltpu.roll(u[3], 32, 1)),
-                jnp.where(even, pltpu.roll(u[2], 96, 1), u[3]),
-            ]
-            for i in range(4):
-                row = (part * 4 + i) * 32
-                x_scr[row : row + 32, e * 32 : e * 32 + 128] = (z[i] * (1.0 / seqs)).astype(
-                    jnp.bfloat16
-                )
+    for part in range(4):
+        block = (c_scr[part].reshape(32, 32, 128) * (1.0 / seqs)).astype(jnp.bfloat16)
+        x_scr[128 * part : 128 * part + 128, :] = jnp.concatenate(
+            [block[:, :, 32 * i : 32 * i + 32].reshape(32, 1024) for i in range(4)], axis=0
+        )
     projected = mm(x_scr[...], project_ref[...])
-    index = lax.broadcasted_iota(jnp.int32, (256, 128), 0)
-    bins = lax.broadcasted_iota(jnp.int32, (256, 128), 1)
-    offset = (c * 32 + index % 32) - (r * 64 + step * 8 + index // 32)
+    index = lax.broadcasted_iota(jnp.int32, (512, 128), 0)
+    bins = lax.broadcasted_iota(jnp.int32, (512, 128), 1)
+    offset = (c * 32 + index % 32) - (r * 64 + step * 16 + index // 32)
     onehot = jnp.where(jnp.clip(offset, -CLIP, CLIP) + CLIP == bins, 1.0, 0.0)
     relative = mm(onehot.astype(jnp.bfloat16), offset_ref[...])
-    left0 = a_ref[2 * step, seqs:, :].astype(jnp.float32)
-    left1 = a_ref[2 * step + 1, seqs:, :].astype(jnp.float32)
-    left = [left0[i : i + 1] for i in range(4)] + [left1[i : i + 1] for i in range(4)]
+    left = []
+    for n in range(4):
+        four = a_ref[4 * step + n, seqs:, :].astype(jnp.float32)
+        left += [four[i : i + 1] for i in range(4)]
     right = right_scr[...]
     embedded = jnp.concatenate([right + one for one in left], axis=0)
     start = embedded + relative + projected
@@ -385,20 +368,20 @@
         mm(standardize_features(start).astype(jnp.bfloat16), expand_ref[...]), 0.0
     ).astype(jnp.bfloat16)
     final = (start + mm(hidden, shrink_ref[...])).astype(jnp.bfloat16)
-    pair_ref[...] = final.reshape(8, 32, 128)
+    pair_ref[...] = final.reshape(16, 32, 128)
     logits = mm(final, bins_ref[...])
     own_scr[step] = logits
-    packed = jnp.where(bins[:128] < 64, logits[:128], logits[128:]).astype(jnp.bfloat16)
+    packed = jnp.where(bins[:256] < 64, logits[:256], logits[256:]).astype(jnp.bfloat16)
     out_scr[step] = packed
 
     @pl.when(stays(step))
     def _():
-        in_scr[parity, step % 4] = packed
+        in_scr[parity, step % 2] = packed
 
     @pl.when(step == pl.num_programs(0) - 1)
     def _():
         dispatch(step)
-        for quarter in range(4):
+        for quarter in range(2):
             for k in range(2):
 
                 @pl.when(jnp.logical_not(jnp.logical_and(diagonal, parity == k)))
@@ -412,17 +395,17 @@
                         device_id_type=MESH,
                     ).wait_recv()
 
-                for i in range(4):
+                for i in range(8):
                     rows = in_scr[k, quarter, 32 * i : 32 * i + 32, :].astype(jnp.float32)
-                    first = k * 1024 + quarter * 8 + i
+                    first = k * 1024 + quarter * 16 + i
                     turn_scr[pl.ds(first, 32, stride=32), :] = rows
-                    turn_scr[pl.ds(first + 4, 32, stride=32), :] = pltpu.roll(rows, 64, 1)
-        for number in range(8):
-            total = own_scr[number] + turn_scr[256 * number : 256 * number + 256, :]
-            distogram_ref[8 * number : 8 * number + 8] = (
-                total[:, :64].astype(jnp.bfloat16).reshape(8, 32, 64)
+                    turn_scr[pl.ds(first + 8, 32, stride=32), :] = pltpu.roll(rows, 64, 1)
+        for number in range(4):
+            total = own_scr[number] + turn_scr[512 * number : 512 * number + 512, :]
+            distogram_ref[16 * number : 16 * number + 16] = (
+                total[:, :64].astype(jnp.bfloat16).reshape(16, 32, 64)
             )
-        for number in range(8):
+        for number in range(4):
 
             @pl.when(jnp.logical_not(stays(number)))
             def _(number=number):
@@ -432,11 +415,11 @@
 def run_pair(a_all, b_all, offset, project, expand, shrink, bins):
     return pl.pallas_call(
         pair_tile,
-        grid=(8,),
+        grid=(4,),
         in_specs=[FULL, FULL]
         + [resident(one.shape) for one in (offset, project, expand, shrink, bins)],
         out_specs=[
-            pl.BlockSpec((8, 32, 128), lambda i: (i, 0, 0)),
+            pl.BlockSpec((16, 32, 128), lambda i: (i, 0, 0)),
             pl.BlockSpec((64, 32, 64), lambda i: (0, 0, 0)),
         ],
         out_shape=[
@@ -444,15 +427,15 @@
             jax.ShapeDtypeStruct((64, 32, 64), jnp.bfloat16),
         ],
         scratch_shapes=[
-            pltpu.VMEM((2, 1024, 128), jnp.float32),
-            pltpu.VMEM((256, 1024), jnp.bfloat16),
+            pltpu.VMEM((4, 1024, 128), jnp.float32),
+            pltpu.VMEM((512, 1024), jnp.bfloat16),
             pltpu.VMEM((32, 128), jnp.float32),
-            pltpu.VMEM((8, 256, 128), jnp.float32),
-            pltpu.VMEM((8, 128, 128), jnp.bfloat16),
-            pltpu.VMEM((2, 4, 128, 128), jnp.bfloat16),
+            pltpu.VMEM((4, 512, 128), jnp.float32),
+            pltpu.VMEM((4, 256, 128), jnp.bfloat16),
+            pltpu.VMEM((2, 2, 256, 128), jnp.bfloat16),
             pltpu.VMEM((2048, 128), jnp.float32),
-            pltpu.SemaphoreType.DMA((8,)),
-            pltpu.SemaphoreType.DMA((2, 4)),
+            pltpu.SemaphoreType.DMA((4,)),
+            pltpu.SemaphoreType.DMA((2, 2)),
         ],
         compiler_params=pltpu.CompilerParams(
             dimension_semantics=("arbitrary",),

time: 127 us -> 120 us (0.945); the launches traced: 127 us -> 118 us
  Pallas kernels: 86.8 us -> 78.1 us
    pallas_call x1, Pallas kernels: 32.6 us -> 23.9 us  [run_pair(): pl.pallas_call(pair_tile, grid=(4,), in_specs=[FULL, FULL] + [resident(on...]
where the time goes in v5:
time: 120 us; the launch traced here: 118 us
  Pallas kernels  78.1 us (65%)
  waiting for transfers between devices  13.8 us (12%)
  local copies, waits for them, and re-layouts  13.3 us (11%)
  starting transfers between devices  10.8 us (9%)
  other arithmetic  1.37 us (1%)
    pallas_call x1, Pallas kernels, run_attention(): pl.pallas_call(column_attention, grid=(count_res,), in_specs=[pl.BlockSpe...  27.5 us
    pallas_call x1, Pallas kernels, run_spread(): pl.pallas_call(spread_factors, in_specs=[FULL, FULL], out_specs=[FULL, FU...  26.7 us
    pallas_call x1, Pallas kernels, run_pair(): pl.pallas_call(pair_tile, grid=(4,), in_specs=[FULL, FULL] + [resident(on...  23.9 us
    all_to_all x1, waiting for transfers between devices, shards(): lax.all_to_all(fragments, ('row', 'col'), split_axis=2, concat_axis=0, ti...  13.8 us
    all_to_all x1, starting transfers between devices, shards(): lax.all_to_all(fragments, ('row', 'col'), split_axis=2, concat_axis=0, ti...  10.8 us
    unnamed x16, local copies, waits for them, and re-layouts  6.92 us
    reshape x1, local copies, waits for them, and re-layouts, shards(): alignment_output = updated.reshape(seqs, res_here, width)  2.63 us
  transfers between devices with their start and end apart: 1, of which 1 were waited for; matrix products, arithmetic and copies ran while one was open for 3% of the time, Pallas kernels for 0%

profile of v5, /device:TPU:7, one launch (start us, length us, event | category | flops | bytes accessed | tf_op | source)
XLA Modules:
  0.0 118.1 jit_solution(8339047817696248748)
XLA Ops:
  0.6 0.0 copy-start.5
  0.6 0.0 copy-start.1
  0.7 0.0 copy-start.2
  0.7 0.0 copy-start.3
  0.7 0.0 copy-start.4
  0.7 0.0 copy-start
  0.7 3.0 %copy.33 = bf16[4,512,256]{2,0,1:T(4,128)(2,1)} copy(bf16[4,512,256]{2,1,0:T(8,128)(2,1)} %param.18) | data formatting | bytes 2097152 | tf_op args[0]
  3.7 10.8 %all-to-all-start = ((bf16[1,4,128,4,256]{4,1,3,0,2:T(4,128)(2,1)}), bf16[1,4,128,4,256]{4,1,3,0,2:T(4,128)(2,1)S(1)}, u32[]{:S(2)}, u32[]{:S(2)}) async-start(bf16[1,4,128,4,256]{4,1,3,0,2:T(4,128)(2,1)} %bitcast), calls=%async_computation | async-start | bytes 2097152 | tf_op jit(solution)/shard_map/all_to_all | solution.py:476
  14.5 0.0 copy-done.5
  14.5 0.6 pad.8.feat_ref
  15.1 0.0 copy-done.1
  15.1 0.6 pad.9.offset_ref
  15.7 0.0 copy-done.2
  15.7 0.1 copy.38
  15.9 0.0 copy-done.3
  15.9 0.1 copy.35
  16.0 0.0 copy-done.4
  16.0 0.1 copy.36
  16.1 0.0 copy-done
  16.1 0.8 copy.37
  17.0 0.7 pad_maximum_fusion.1.bins_ref
  17.7 0.7 pad_maximum_fusion.factor_ref
  18.3 13.8 %all-to-all-done = bf16[1,4,128,4,256]{4,1,3,0,2:T(4,128)(2,1)S(1)} async-done(((bf16[1,4,128,4,256]{4,1,3,0,2:T(4,128)(2,1)}), bf16[1,4,128,4,256]{4,1,3,0,2:T(4,128)(2,1)S(1)}, u32[]{:S(2)}, u32[]{:S(2)}) %all-to-all-start) | async-done | bytes 1048608 | tf_op jit(solution)/shard_map/all_to_all | solution.py:476
  32.2 0.4 copy.34
  32.5 1.1 reshape.31
  33.6 27.5 %column_attention.1 = (bf16[512,1024]{1,0:T(8,128)(2,1)}, bf16[528,128]{1,0:T(8,128)(2,1)}, bf16[144,512]{1,0:T(8,128)(2,1)}) custom-call(bf16[4,512,256]{2,1,0:T(8,128)(2,1)} %bitcast.13, bf16[16,256]{1,0:T(8,128)(2,1)} %pad.8.feat_ref, bf16[256,256]{1,0:T(8,128)(2,1)} %wq_ref.1, bf16[256,256]{1,0:T(8,128)(2,1)} %wk_ref.1, bf16[256,256]{1,0:T(8,128)(2,1)} %wv_ref.1, ...), custom_call_target="tpu_custom_call" | custom-call | tf_op jit(solution)/shard_map/column_attention/pallas_call | solution.py:118
  61.1 2.6 %reshape.32 = bf16[512,4,256]{2,1,0:T(4,128)(2,1)} reshape(bf16[512,1024]{1,0:T(8,128)(2,1)} %get-tuple-element.10) | data formatting | bytes 2097152 | tf_op jit(solution)/shard_map/reshape | solution.py:498
  63.8 26.7 %spread_factors.1 = (bf16[16,528,128]{2,1,0:T(8,128)(2,1)}, bf16[8,144,512]{2,1,0:T(8,128)(2,1)}) custom-call(bf16[528,128]{1,0:T(8,128)(2,1)} %get-tuple-element.11.a_ref, bf16[144,512]{1,0:T(8,128)(2,1)} %get-tuple-element.12.b_ref), custom_call_target="tpu_custom_call" | custom-call | tf_op jit(solution)/shard_map/spread_factors/pallas_call | solution.py:257
  90.5 23.9 %pair_tile.1 = (bf16[64,32,128]{2,1,0:T(8,128)(2,1)}, bf16[64,32,64]{2,1,0:T(8,128)(2,1)}) custom-call(bf16[16,528,128]{2,1,0:T(8,128)(2,1)} %get-tuple-element.13.a_ref, bf16[8,144,512]{2,1,0:T(8,128)(2,1)} %get-tuple-element.14.b_ref, bf16[128,128]{1,0:T(8,128)(2,1)} %pad.9.offset_ref, bf16[1024,128]{1,0:T(8,128)(2,1)} %bitcast.15, ...), custom_call_target="tpu_custom_call" | custom-call | tf_op jit(solution)/shard_map/pair_tile/pallas_call | solution.py:416
  114.4 1.9 %copy.42 = bf16[64,32,128]{2,1,0:T(8,128)(2,1)} copy(bf16[64,32,128]{2,1,0:T(8,128)(2,1)} %get-tuple-element.21) | data formatting | bytes 1048576
  116.3 1.9 %copy.43 = bf16[64,32,64]{2,1,0:T(8,128)(2,1)} copy(bf16[64,32,64]{2,1,0:T(8,128)(2,1)} %get-tuple-element.22) | data formatting | bytes 524288
  (2 shorter events, 0.0 us)
Async XLA Ops:
  0.6 13.9 %copy-start.5 = (bf16[4,256]{1,0:T(4,128)(2,1)S(1)}, bf16[4,256]{1,0:T(4,128)(2,1)}, u32[]{:S(2)}) copy-start(bf16[4,256]{1,0:T(4,128)(2,1)} %param.19) | copy-start | bytes 6148
  0.6 14.5 %copy-start.1 = (bf16[65,128]{1,0:T(8,128)(2,1)S(1)}, bf16[65,128]{1,0:T(8,128)(2,1)}, u32[]{:S(2)}) copy-start(bf16[65,128]{1,0:T(8,128)(2,1)} %param.32) | copy-start | bytes 49924
  0.7 15.1 %copy-start.2 = (bf16[128,64]{0,1:T(8,128)(2,1)S(1)}, bf16[128,64]{0,1:T(8,128)(2,1)}, u32[]{:S(2)}) copy-start(bf16[128,64]{0,1:T(8,128)(2,1)} %param.35) | copy-start | bytes 49156
  0.7 15.2 %copy-start.3 = (bf16[256,32]{0,1:T(8,128)(2,1)S(1)}, bf16[256,32]{0,1:T(8,128)(2,1)}, u32[]{:S(2)}) copy-start(bf16[256,32]{0,1:T(8,128)(2,1)} %param.27) | copy-start | bytes 49156
  0.7 15.3 %copy-start.4 = (bf16[256,32]{0,1:T(8,128)(2,1)S(1)}, bf16[256,32]{0,1:T(8,128)(2,1)}, u32[]{:S(2)}) copy-start(bf16[256,32]{0,1:T(8,128)(2,1)} %param.28) | copy-start | bytes 49156
  0.7 15.5 %copy-start = (bf16[1024,128]{1,0:T(8,128)(2,1)S(1)}, bf16[1024,128]{1,0:T(8,128)(2,1)}, u32[]{:S(2)}) copy-start(bf16[1024,128]{1,0:T(8,128)(2,1)} %param.29) | copy-start | bytes 786436
  3.7 28.4 %all-to-all-start = ((bf16[1,4,128,4,256]{4,1,3,0,2:T(4,128)(2,1)}), bf16[1,4,128,4,256]{4,1,3,0,2:T(4,128)(2,1)S(1)}, u32[]{:S(2)}, u32[]{:S(2)}) async-start(bf16[1,4,128,4,256]{4,1,3,0,2:T(4,128)(2,1)} %bitcast), calls=%async_computation | async-start | bytes 2097152 | tf_op jit(solution)/shard_map/all_to_all | solution.py:476

commit v6 on v5

--- a/solution.py
+++ b/solution.py
@@ -29,6 +29,135 @@
 
 def mm(a, b):
     return jnp.dot(a, b, preferred_element_type=jnp.float32)
+
+
+class Spread:
+    def __init__(self, own, a_all, b_all, a_send, a_recv, b_send, b_recv):
+        self.own, self.a_all, self.b_all = own, a_all, b_all
+        self.a_send, self.a_recv, self.b_send, self.b_recv = a_send, a_recv, b_send, b_recv
+        self.rows, cols = lax.axis_size("row"), lax.axis_size("col")
+        self.half = cols // 2
+        r, c = lax.axis_index("row"), lax.axis_index("col")
+        high, within = c // self.half, c % self.half
+        self.r, self.c, self.within = r, c, within
+        self.turned = 1 - 2 * (c % 2)
+        self.mate = c + self.turned
+        self.other_high = (1 - high) * self.half + within
+        self.other_row = r + 1 - 2 * (r % 2)
+        self.ahead = 2 * self.turned
+        self.first_dest = (within + 1 - 2 * (within % 2), 2 * r + high)
+        self.first_origin = (c // 2, c % 2 * self.half + self.other_row)
+
+    def along_x(self, column, shift):
+        half = self.half
+        return column // half * half + (column % half + shift + half) % half
+
+    def along_y(self, row, shift):
+        return (row + shift + self.rows) % self.rows
+
+    def greet(self):
+        barrier = pltpu.get_barrier_semaphore()
+        r, c = self.r, self.c
+        peers = [
+            (r, self.mate),
+            (r, self.other_high),
+            (r, self.along_x(c, 2)),
+            (r, self.along_x(c, -2)),
+            (self.other_row, c),
+            (self.along_y(r, 2), c),
+            (self.along_y(r, -2), c),
+            self.first_dest,
+            self.first_origin,
+        ]
+        for peer in peers:
+            pl.semaphore_signal(barrier, inc=1, device_id=peer, device_id_type=MESH)
+        pl.semaphore_wait(barrier, len(peers))
+
+    def copy_a(self, part, slot, number, column):
+        return pltpu.make_async_remote_copy(
+            src_ref=self.a_all.at[slot, part],
+            dst_ref=self.a_all.at[slot, part],
+            send_sem=self.a_send.at[part, number],
+            recv_sem=self.a_recv.at[part, slot],
+            device_id=(self.r, column),
+            device_id_type=MESH,
+        )
+
+    def copy_b(self, part, slot, number, device, src=None):
+        return pltpu.make_async_remote_copy(
+            src_ref=self.b_all.at[slot, part] if src is None else src,
+            dst_ref=self.b_all.at[slot, part],
+            send_sem=self.b_send.at[part, number],
+            recv_sem=self.b_recv.at[part, slot],
+            device_id=device,
+            device_id_type=MESH,
+        )
+
+    def wait_a(self, part, slot):
+        self.copy_a(part, slot, 0, self.mate).wait_recv()
+
+    def wait_b(self, part, slot):
+        self.copy_b(part, slot, 0, (self.other_row, self.c)).wait_recv()
+
+    def begin(self, part):
+        c, ahead = self.c, self.ahead
+        self.copy_b(part, self.within, 0, self.first_dest, self.own.at[part]).start()
+        self.copy_a(part, c, 0, self.other_high).start()
+        self.copy_a(part, c, 1, self.along_x(c, ahead)).start()
+        self.copy_a(part, c, 2, self.along_x(c, -ahead)).start()
+        self.copy_a(part, c, 3, self.mate).start()
+
+    def second(self, part):
+        r, c, ahead, kept = self.r, self.c, self.ahead, self.other_row
+        self.wait_b(part, kept)
+        self.copy_b(part, kept, 1, (self.other_row, c)).start()
+        self.copy_b(part, kept, 2, (self.along_y(r, ahead), c)).start()
+        self.copy_b(part, kept, 3, (self.along_y(r, -ahead), c)).start()
+        self.wait_a(part, self.other_high)
+        self.copy_a(part, self.other_high, 4, self.along_x(c, ahead)).start()
+        self.copy_a(part, self.other_high, 5, self.along_x(c, -ahead)).start()
+        self.copy_a(part, self.other_high, 6, self.mate).start()
+
+    def third(self, part):
+        r, c, ahead = self.r, self.c, self.ahead
+        self.wait_b(part, r)
+        self.copy_b(part, r, 4, (self.along_y(r, ahead), c)).start()
+        self.copy_b(part, r, 5, (self.along_y(r, -ahead), c)).start()
+        self.relay(part, 0, c, self.other_row)
+
+    def fourth(self, part):
+        self.relay(part, 1, self.other_high, self.r)
+
+    def relay(self, part, turn, a_slot, b_slot):
+        r, c, ahead = self.r, self.c, self.ahead
+        back = self.along_x(a_slot, -ahead)
+        self.wait_a(part, back)
+        self.copy_a(part, back, 7 + 4 * turn, self.along_x(c, ahead)).start()
+        self.copy_a(part, back, 8 + 4 * turn, self.mate).start()
+        behind = self.along_y(b_slot, -ahead)
+        self.wait_b(part, behind)
+        self.copy_b(part, behind, 6 + turn, (self.along_y(r, ahead), c)).start()
+        front = self.along_x(a_slot, ahead)
+        self.wait_a(part, front)
+        self.copy_a(part, front, 9 + 4 * turn, self.mate).start()
+
+    def fifth(self, part):
+        for turn, a_slot in enumerate((self.c, self.other_high)):
+            far = self.along_x(a_slot, 4)
+            self.wait_a(part, far)
+            self.copy_a(part, far, 10 + 4 * turn, self.mate).start()
+
+    def finish(self, part):
+        for b_slot in (self.other_row, self.r):
+            self.wait_b(part, self.along_y(b_slot, self.ahead))
+            self.wait_b(part, self.along_y(b_slot, 4))
+        for a_slot in (self.c, self.other_high):
+            for shift in range(0, self.half, 2):
+                self.wait_a(part, self.along_x(a_slot + self.turned, shift))
+        for number in range(15):
+            self.copy_a(part, self.c, number, self.mate).wait_send()
+        for number in range(8):
+            self.copy_b(part, self.r, number, (self.other_row, self.c)).wait_send()
 
 
 def column_attention(
@@ -45,16 +174,35 @@
     row_ref,
     column_ref,
     out_ref,
-    a_ref,
-    b_ref,
+    a_out,
+    b_out,
     q_scr,
     kt_scr,
     v_scr,
     acc_scr,
-    fac_scr,
+    own_scr,
+    a_all,
+    b_all,
+    a_send,
+    a_recv,
+    b_send,
+    b_recv,
+    out_sem,
 ):
     step = pl.program_id(0)
     seqs = x_ref.shape[1]
+    spread = Spread(own_scr, a_all, b_all, a_send, a_recv, b_send, b_recv)
+
+    @pl.when(step == 0)
+    def _():
+        feat = feat_ref[...]
+        a_all[spread.c, 0] = jnp.zeros((32, seqs), jnp.bfloat16)
+        own_scr[0] = jnp.zeros((32, seqs), jnp.bfloat16)
+        a_all[spread.c, 0, :16, :128] = mm(feat, row_ref[...]).astype(jnp.bfloat16)
+        own_scr[0, :16, :128] = mm(feat, column_ref[...]).astype(jnp.bfloat16)
+        spread.greet()
+
+    spread.begin(step)
     x = x_ref[0].astype(jnp.float32)
     normed = standardize_features(x).astype(jnp.bfloat16)
     q_scr[...] = mm(normed, wq_ref[...]).astype(jnp.bfloat16)
@@ -66,7 +214,7 @@
     lane = lax.broadcasted_iota(jnp.int32, (seqs, 256), 1)
     factor = math.log2(math.e) / math.sqrt(HEAD)
 
-    def one_group(group, carry):
+    for group in range(2):
         total = None
         for k in range(HEADS // 2):
             q = jnp.where(
@@ -81,9 +229,6 @@
             part = mm(weights, values)
             total = part if total is None else total + part
         acc_scr[group] = total
-        return carry
-
-    lax.fori_loop(0, 2, one_group, 0)
     attended = jnp.concatenate(
         [
             acc_scr[0, :, :128] / acc_scr[0, :, 128:],
@@ -100,16 +245,48 @@
     second = first + mm(hidden, ws_ref[...])
     out_ref[...] = second.astype(jnp.bfloat16)
     factors = mm(standardize_features(second).astype(jnp.bfloat16), factor_ref[...])
-    fac_scr[...] = jnp.where(lane % 128 // HEAD == step, factors, fac_scr[...])
-
-    @pl.when(step == pl.num_programs(0) - 1)
-    def _():
-        a_ref[:seqs, :] = fac_scr[:, :128].astype(jnp.bfloat16)
-        b_ref[:128, :] = fac_scr[:, 128:].T.astype(jnp.bfloat16)
-        feat = feat_ref[...]
-        a_ref[seqs:, :] = mm(feat, row_ref[...]).astype(jnp.bfloat16)
-        b_ref[128:, :128] = mm(feat, column_ref[...]).astype(jnp.bfloat16)
-        b_ref[128:, 128:] = jnp.zeros((16, seqs - 128), jnp.bfloat16)
+    turned = factors.T.astype(jnp.bfloat16)
+    a_all[spread.c, step + 1] = turned[:32]
+    own_scr[step + 1] = turned[32:64]
+    spread.second(step)
+
+    @pl.when(step > 0)
+    def _():
+        spread.third(step - 1)
+
+    @pl.when(step > 1)
+    def _():
+        spread.fourth(step - 2)
+
+    @pl.when(step > 2)
+    def _():
+        spread.fifth(step - 3)
+
+    last = pl.num_programs(0)
+
+    @pl.when(step == last - 1)
+    def _():
+        spread.begin(last)
+        spread.third(last - 1)
+        spread.fourth(last - 2)
+        spread.fifth(last - 3)
+        spread.second(last)
+        spread.fourth(last - 1)
+        spread.fifth(last - 2)
+        spread.third(last)
+        spread.fifth(last - 1)
+        spread.fourth(last)
+        spread.fifth(last)
+        for part in range(5):
+            spread.finish(part)
+        results = [
+            pltpu.make_async_copy(a_all, a_out, out_sem.at[0]),
+            pltpu.make_async_copy(b_all, b_out, out_sem.at[1]),
+        ]
+        for copy in results:
+            copy.start()
+        for copy in results:
+            copy.wait()
 
 
 def run_attention(x, feat, weights, interpret=False):
@@ -121,156 +298,36 @@
         in_specs=[pl.BlockSpec((1, seqs, width), lambda i: (i, 0, 0))] + whole,
         out_specs=[
             pl.BlockSpec((seqs, width), lambda i: (0, i)),
-            FULL,
-            FULL,
+            pl.BlockSpec(memory_space=pl.ANY),
+            pl.BlockSpec(memory_space=pl.ANY),
         ],
         out_shape=[
             jax.ShapeDtypeStruct((seqs, count_res * width), jnp.bfloat16),
-            jax.ShapeDtypeStruct((seqs + 16, 128), jnp.bfloat16),
-            jax.ShapeDtypeStruct((144, seqs), jnp.bfloat16),
+            jax.ShapeDtypeStruct((16, count_res + 1, 32, seqs), jnp.bfloat16),
+            jax.ShapeDtypeStruct((8, count_res + 1, 32, seqs), jnp.bfloat16),
         ],
         scratch_shapes=[
             pltpu.VMEM((seqs, width), jnp.bfloat16),
             pltpu.VMEM((width, seqs), jnp.bfloat16),
             pltpu.VMEM((2, seqs, width), jnp.bfloat16),
             pltpu.VMEM((2, seqs, width), jnp.float32),
-            pltpu.VMEM((seqs, width), jnp.float32),
+            pltpu.VMEM((count_res + 1, 32, seqs), jnp.bfloat16),
+            pltpu.VMEM((16, count_res + 1, 32, seqs), jnp.bfloat16),
+            pltpu.VMEM((8, count_res + 1, 32, seqs), jnp.bfloat16),
+            pltpu.SemaphoreType.DMA((count_res + 1, 15)),
+            pltpu.SemaphoreType.DMA((count_res + 1, 16)),
+            pltpu.SemaphoreType.DMA((count_res + 1, 8)),
+            pltpu.SemaphoreType.DMA((count_res + 1, 8)),
+            pltpu.SemaphoreType.DMA((2,)),
         ],
         compiler_params=pltpu.CompilerParams(
-            dimension_semantics=("arbitrary",), vmem_limit_bytes=VMEM_LIMIT
+            dimension_semantics=("arbitrary",),
+            vmem_limit_bytes=VMEM_LIMIT,
+            collective_id=0,
+            has_side_effects=True,
         ),
         name="column_attention",
     )(x, feat, *weights)
-
-
-def spread_factors(a_ref, b_ref, a_all, b_all, a_send, a_recv, b_send, b_recv):
-    rows, cols = lax.axis_size("row"), lax.axis_size("col")
-    half = cols // 2
-    r, c = lax.axis_index("row"), lax.axis_index("col")
-    high, within = c // half, c % half
-    core = c % 2
-    other_core = c + 1 - 2 * core
-    other_high = (1 - high) * half + within
-    other_row = r + 1 - 2 * (r % 2)
-    ahead = 2 - 4 * core
-
-    def along_x(column, shift):
-        return column // half * half + (column % half + shift + half) % half
-
-    def along_y(row, shift):
-        return (row + shift + rows) % rows
-
-    spot = within + 1 - 2 * (within % 2)
-    first_dest = (spot, 2 * r + high)
-    kept = other_row
-    first_origin = (c // 2, c % 2 * half + kept)
-    barrier = pltpu.get_barrier_semaphore()
-    peers = [
-        (r, other_core),
-        (r, other_high),
-        (r, along_x(c, 2)),
-        (r, along_x(c, -2)),
-        (other_row, c),
-        (along_y(r, 2), c),
-        (along_y(r, -2), c),
-        first_dest,
-        first_origin,
-    ]
-    for peer in peers:
-        pl.semaphore_signal(barrier, inc=1, device_id=peer, device_id_type=MESH)
-    pl.semaphore_wait(barrier, len(peers))
-    sent = []
-
-    def send(src, full, slot, sends, recvs, number, device):
-        copy = pltpu.make_async_remote_copy(
-            src_ref=src,
-            dst_ref=full.at[slot],
-            send_sem=sends.at[number],
-            recv_sem=recvs.at[slot],
-            device_id=device,
-            device_id_type=MESH,
-        )
-        copy.start()
-        sent.append(copy)
-
-    def send_a(src, slot, number, column):
-        send(src, a_all, slot, a_send, a_recv, number, (r, column))
-
-    def send_b(src, slot, number, device):
-        send(src, b_all, slot, b_send, b_recv, number, device)
-
-    def arrived(full, slot, recvs):
-        pltpu.make_async_remote_copy(
-            src_ref=full.at[slot],
-            dst_ref=full.at[slot],
-            send_sem=recvs.at[slot],
-            recv_sem=recvs.at[slot],
-            device_id=(r, other_core),
-            device_id_type=MESH,
-        ).wait_recv()
-
-    send_b(b_ref, within, 0, first_dest)
-    send_a(a_ref, c, 0, other_high)
-    send_a(a_ref, c, 1, along_x(c, ahead))
-    send_a(a_ref, c, 2, along_x(c, -ahead))
-    send_a(a_ref, c, 3, other_core)
-    a_all[c] = a_ref[...]
-    arrived(b_all, kept, b_recv)
-    send_b(b_all.at[kept], kept, 1, (other_row, c))
-    send_b(b_all.at[kept], kept, 2, (along_y(r, ahead), c))
-    send_b(b_all.at[kept], kept, 3, (along_y(r, -ahead), c))
-    arrived(a_all, other_high, a_recv)
-    send_a(a_all.at[other_high], other_high, 4, along_x(c, ahead))
-    send_a(a_all.at[other_high], other_high, 5, along_x(c, -ahead))
-    send_a(a_all.at[other_high], other_high, 6, other_core)
-    arrived(b_all, r, b_recv)
-    send_b(b_all.at[r], r, 4, (along_y(r, ahead), c))
-    send_b(b_all.at[r], r, 5, (along_y(r, -ahead), c))
-    for turn, (a_slot, b_slot) in enumerate(((c, kept), (other_high, r))):
-        back = along_x(a_slot, -ahead)
-        arrived(a_all, back, a_recv)
-        send_a(a_all.at[back], back, 7 + 4 * turn, along_x(c, ahead))
-        send_a(a_all.at[back], back, 8 + 4 * turn, other_core)
-        behind = along_y(b_slot, -ahead)
-        arrived(b_all, behind, b_recv)
-        send_b(b_all.at[behind], behind, 6 + turn, (along_y(r, ahead), c))
-        front = along_x(a_slot, ahead)
-        arrived(a_all, front, a_recv)
-        send_a(a_all.at[front], front, 9 + 4 * turn, other_core)
-    for turn, a_slot in enumerate((c, other_high)):
-        far = along_x(a_slot, 4)
-        arrived(a_all, far, a_recv)
-        send_a(a_all.at[far], far, 10 + 4 * turn, other_core)
-    for b_slot in (kept, r):
-        arrived(b_all, along_y(b_slot, ahead), b_recv)
-        arrived(b_all, along_y(b_slot, 4), b_recv)
-    for a_slot in (c, other_high):
-        mate = a_slot + 1 - 2 * core
-        for shift in range(0, half, 2):
-            arrived(a_all, along_x(mate, shift), a_recv)
-    for copy in sent:
-        copy.wait_send()
-
-
-def run_spread(a_block, b_block, rows, cols):
-    half = cols // 2
-    return pl.pallas_call(
-        spread_factors,
-        in_specs=[FULL, FULL],
-        out_specs=[FULL, FULL],
-        out_shape=[
-            jax.ShapeDtypeStruct((cols,) + a_block.shape, jnp.bfloat16),
-            jax.ShapeDtypeStruct((half,) + b_block.shape, jnp.bfloat16),
-        ],
-        scratch_shapes=[
-            pltpu.SemaphoreType.DMA((15,)),
-            pltpu.SemaphoreType.DMA((cols,)),
-            pltpu.SemaphoreType.DMA((8,)),
-            pltpu.SemaphoreType.DMA((half,)),
-        ],
-        compiler_params=pltpu.CompilerParams(collective_id=0, has_side_effects=True),
-        name="spread_factors",
-    )(a_block, b_block)
 
 
 def pair_tile(
@@ -294,7 +351,7 @@
     recv_sem,
 ):
     step = pl.program_id(0)
-    seqs = b_ref.shape[2]
+    seqs = b_ref.shape[3]
     r, c = lax.axis_index("row"), lax.axis_index("col")
     mirror_row, parity = c // 2, c % 2
     diagonal = mirror_row == r
@@ -335,10 +392,15 @@
     @pl.when(step == 0)
     def _():
         for d in range(8):
-            right_scr[4 * d : 4 * d + 4, :] = b_ref[d, 128:, :128].astype(jnp.float32)[:4]
-
-    factors = jnp.concatenate([a_ref[4 * step + n, :seqs, :] for n in range(4)], axis=1)
-    outer = mm(b_ref[:, :128, :].reshape(1024, seqs), factors)
+            right_scr[4 * d : 4 * d + 4, :] = b_ref[d, 0, :16, :128].astype(jnp.float32)[:4]
+
+    factors = a_ref[pl.ds(4 * step, 4), 1:].reshape(512, seqs)
+    outer = lax.dot_general(
+        b_ref[:, 1:].reshape(1024, seqs),
+        factors,
+        (((1,), (1,)), ((), ())),
+        preferred_element_type=jnp.float32,
+    )
     for part in range(4):
         c_scr[part] = outer[:, 128 * part : 128 * part + 128]
 
@@ -359,7 +421,7 @@
     relative = mm(onehot.astype(jnp.bfloat16), offset_ref[...])
     left = []
     for n in range(4):
-        four = a_ref[4 * step + n, seqs:, :].astype(jnp.float32)
+        four = a_ref[4 * step + n, 0, :16, :128].astype(jnp.float32)
         left += [four[i : i + 1] for i in range(4)]
     right = right_scr[...]
     embedded = jnp.concatenate([right + one for one in left], axis=0)
@@ -477,9 +539,9 @@
     local = moved.reshape(-1, res_here, width)
     seqs = local.shape[0]
     both = jnp.concatenate(
-        [jnp.tile(former_factor_matrix, (1, 4)), jnp.tile(latter_factor_matrix, (1, 4))], axis=1
-    )
-    updated, a_block, b_block = run_attention(
+        [former_factor_matrix, latter_factor_matrix, jnp.zeros((width, 64), jnp.bfloat16)], axis=1
+    )
+    updated, a_all, b_all = run_attention(
         local.transpose(1, 0, 2),
         jnp.pad(per_amino_features, ((0, 12), (0, 0))),
         (
@@ -496,7 +558,6 @@
         ),
     )
     alignment_output = updated.reshape(seqs, res_here, width)
-    a_all, b_all = run_spread(a_block, b_block, rows, cols)
     factor = former_factor_matrix.shape[1]
     project = (
         factor_mean_projection.reshape(factor, factor, -1)

time: 120 us -> 110 us (0.917)
  Pallas kernels: 78.1 us -> 68.8 us
    pallas_call x1 -> x0, Pallas kernels: 26.7 us -> none  [run_spread(): pl.pallas_call(spread_factors, in_specs=[FULL, FULL], out_specs=[FULL, FU...]
    pallas_call x1, Pallas kernels: 27.5 us -> 44.4 us  [run_attention(): pl.pallas_call(column_attention, grid=(count_res,), in_specs=[pl.BlockSpe...]
    unnamed x16 -> x18, local copies, waits for them, and re-layouts: 6.92 us -> 7.16 us
  transfers between devices with their start and end apart: 1 -> 1, of which waited for: 1 -> 1; matrix products, arithmetic and copies ran while one was open for 3% -> 4% of each run, Pallas kernels for 0% -> 0%
where the time goes in v6:
time: 110 us; the launch traced here: 109 us
  Pallas kernels  68.8 us (63%)
  waiting for transfers between devices  13.8 us (13%)
  local copies, waits for them, and re-layouts  13.4 us (12%)
  starting transfers between devices  10.8 us (10%)
  other arithmetic  1.41 us (1%)
    pallas_call x1, Pallas kernels, run_attention(): pl.pallas_call(column_attention, grid=(count_res,), in_specs=[pl.BlockSpe...  44.4 us
    pallas_call x1, Pallas kernels, run_pair(): pl.pallas_call(pair_tile, grid=(4,), in_specs=[FULL, FULL] + [resident(on...  24.4 us
    all_to_all x1, waiting for transfers between devices, shards(): lax.all_to_all(fragments, ('row', 'col'), split_axis=2, concat_axis=0, ti...  13.8 us
    all_to_all x1, starting transfers between devices, shards(): lax.all_to_all(fragments, ('row', 'col'), split_axis=2, concat_axis=0, ti...  10.8 us
    unnamed x18, local copies, waits for them, and re-layouts  7.16 us
    reshape x1, local copies, waits for them, and re-layouts, shards(): alignment_output = updated.reshape(seqs, res_here, width)  2.64 us
  transfers between devices with their start and end apart: 1, of which 1 were waited for; matrix products, arithmetic and copies ran while one was open for 4% of the time, Pallas kernels for 0%

profile of v6, /device:TPU:7, one launch (start us, length us, event | category | flops | bytes accessed | tf_op | source)
XLA Modules:
  0.0 108.8 jit_solution(18032539732136484978)
XLA Ops:
  0.6 0.0 copy-start.2
  0.6 0.0 copy-start.3
  0.7 0.0 copy-start.5
  0.7 0.0 copy-start.1
  0.7 0.0 copy-start
  0.7 0.0 copy-start.4
  0.7 3.0 %copy.27 = bf16[4,512,256]{2,0,1:T(4,128)(2,1)} copy(bf16[4,512,256]{2,1,0:T(8,128)(2,1)} %param.18) | data formatting | bytes 2097152 | tf_op args[0]
  3.7 10.8 %all-to-all-start = ((bf16[1,4,128,4,256]{4,1,3,0,2:T(4,128)(2,1)}), bf16[1,4,128,4,256]{4,1,3,0,2:T(4,128)(2,1)S(1)}, u32[]{:S(2)}, u32[]{:S(2)}) async-start(bf16[1,4,128,4,256]{4,1,3,0,2:T(4,128)(2,1)} %bitcast), calls=%async_computation | async-start | bytes 2097152 | tf_op jit(solution)/shard_map/all_to_all | solution.py:538
  14.5 0.0 copy-done.2
  14.5 0.1 copy.30
  14.6 0.0 copy-done.3
  14.6 0.1 copy.29
  14.8 0.0 copy-done.5
  14.8 0.6 pad.8.feat_ref
  15.4 0.0 copy-done.1
  15.4 0.6 pad.9.offset_ref
  16.0 0.0 copy-done
  16.0 0.8 copy.31
  16.8 0.0 copy-done.4
  16.8 0.1 copy.32
  16.9 0.1 pad.14.clone
  17.0 0.7 pad_maximum_fusion.bins_ref
  17.7 0.7 maximum_maximum_fusion.factor_ref
  18.4 13.8 %all-to-all-done = bf16[1,4,128,4,256]{4,1,3,0,2:T(4,128)(2,1)S(1)} async-done(((bf16[1,4,128,4,256]{4,1,3,0,2:T(4,128)(2,1)}), bf16[1,4,128,4,256]{4,1,3,0,2:T(4,128)(2,1)S(1)}, u32[]{:S(2)}, u32[]{:S(2)}) %all-to-all-start) | async-done | bytes 1048608 | tf_op jit(solution)/shard_map/all_to_all | solution.py:538
  32.2 0.4 copy.28
  32.5 1.1 %reshape.23 = bf16[512,4,256]{2,0,1:T(8,128)(2,1)} reshape(bf16[128,1,4,1,4,256]{5,2,0,4,3,1:T(4,128)(2,1)S(1)} %copy.28) | data formatting | bytes 2097152 | tf_op jit(solution)/shard_map/reshape | solution.py:539
  33.6 44.4 %column_attention.1 = (bf16[512,1024]{1,0:T(8,128)(2,1)}, bf16[16,5,32,512]{3,2,1,0:T(8,128)(2,1)}, bf16[8,5,32,512]{3,2,1,0:T(8,128)(2,1)}) custom-call(bf16[4,512,256]{2,1,0:T(8,128)(2,1)} %bitcast.11, bf16[16,256]{1,0:T(8,128)(2,1)} %pad.8.feat_ref, bf16[256,256]{1,0:T(8,128)(2,1)} %wq_ref.1, bf16[256,256]{1,0:T(8,128)(2,1)} %wk_ref.1, ...), custom_call_target="tpu_custom_call" | custom-call | tf_op jit(solution)/shard_map/column_attention/pallas_call | solution.py:295
  78.0 2.6 %reshape.24 = bf16[512,4,256]{2,1,0:T(4,128)(2,1)} reshape(bf16[512,1024]{1,0:T(8,128)(2,1)} %get-tuple-element.8) | data formatting | bytes 2097152 | tf_op jit(solution)/shard_map/reshape | solution.py:560
  80.6 24.4 %pair_tile.1 = (bf16[64,32,128]{2,1,0:T(8,128)(2,1)}, bf16[64,32,64]{2,1,0:T(8,128)(2,1)}) custom-call(bf16[16,5,32,512]{3,2,1,0:T(8,128)(2,1)} %get-tuple-element.9.a_ref, bf16[8,5,32,512]{3,2,1,0:T(8,128)(2,1)} %get-tuple-element.10.b_ref, bf16[128,128]{1,0:T(8,128)(2,1)} %pad.9.offset_ref, bf16[1024,128]{1,0:T(8,128)(2,1)} %bitcast.13, ...), custom_call_target="tpu_custom_call" | custom-call | tf_op jit(solution)/shard_map/pair_tile/pallas_call | solution.py:478
  105.1 1.9 %copy.36 = bf16[64,32,128]{2,1,0:T(8,128)(2,1)} copy(bf16[64,32,128]{2,1,0:T(8,128)(2,1)} %get-tuple-element.17) | data formatting | bytes 1048576
  106.9 1.9 %copy.37 = bf16[64,32,64]{2,1,0:T(8,128)(2,1)} copy(bf16[64,32,64]{2,1,0:T(8,128)(2,1)} %get-tuple-element.18) | data formatting | bytes 524288
  (1 shorter events, 0.0 us)
Async XLA Ops:
  0.6 13.9 %copy-start.2 = (bf16[256,32]{0,1:T(8,128)(2,1)S(1)}, bf16[256,32]{0,1:T(8,128)(2,1)}, u32[]{:S(2)}) copy-start(bf16[256,32]{0,1:T(8,128)(2,1)} %param.28) | copy-start | bytes 49156
  0.6 14.0 %copy-start.3 = (bf16[256,32]{0,1:T(8,128)(2,1)S(1)}, bf16[256,32]{0,1:T(8,128)(2,1)}, u32[]{:S(2)}) copy-start(bf16[256,32]{0,1:T(8,128)(2,1)} %param.27) | copy-start | bytes 49156
  0.7 14.1 %copy-start.5 = (bf16[4,256]{1,0:T(4,128)(2,1)S(1)}, bf16[4,256]{1,0:T(4,128)(2,1)}, u32[]{:S(2)}) copy-start(bf16[4,256]{1,0:T(4,128)(2,1)} %param.19) | copy-start | bytes 6148
  0.7 14.7 %copy-start.1 = (bf16[65,128]{1,0:T(8,128)(2,1)S(1)}, bf16[65,128]{1,0:T(8,128)(2,1)}, u32[]{:S(2)}) copy-start(bf16[65,128]{1,0:T(8,128)(2,1)} %param.32) | copy-start | bytes 49924
  0.7 15.3 %copy-start = (bf16[1024,128]{1,0:T(8,128)(2,1)S(1)}, bf16[1024,128]{1,0:T(8,128)(2,1)}, u32[]{:S(2)}) copy-start(bf16[1024,128]{1,0:T(8,128)(2,1)} %param.29) | copy-start | bytes 786436
  0.7 16.1 %copy-start.4 = (bf16[128,64]{0,1:T(8,128)(2,1)S(1)}, bf16[128,64]{0,1:T(8,128)(2,1)}, u32[]{:S(2)}) copy-start(bf16[128,64]{0,1:T(8,128)(2,1)} %param.35) | copy-start | bytes 49156
  3.7 28.4 %all-to-all-start = ((bf16[1,4,128,4,256]{4,1,3,0,2:T(4,128)(2,1)}), bf16[1,4,128,4,256]{4,1,3,0,2:T(4,128)(2,1)S(1)}, u32[]{:S(2)}, u32[]{:S(2)}) async-start(bf16[1,4,128,4,256]{4,1,3,0,2:T(4,128)(2,1)} %bitcast), calls=%async_computation | async-start | bytes 2097152 | tf_op jit(solution)/shard_map/all_to_all | solution.py:538

commit v7 on v6

--- a/solution.py
+++ b/solution.py
@@ -201,8 +201,8 @@
         a_all[spread.c, 0, :16, :128] = mm(feat, row_ref[...]).astype(jnp.bfloat16)
         own_scr[0, :16, :128] = mm(feat, column_ref[...]).astype(jnp.bfloat16)
         spread.greet()
-
-    spread.begin(step)
+        spread.begin(0)
+
     x = x_ref[0].astype(jnp.float32)
     normed = standardize_features(x).astype(jnp.bfloat16)
     q_scr[...] = mm(normed, wq_ref[...]).astype(jnp.bfloat16)
@@ -249,6 +249,7 @@
     a_all[spread.c, step + 1] = turned[:32]
     own_scr[step + 1] = turned[32:64]
     spread.second(step)
+    spread.begin(step + 1)
 
     @pl.when(step > 0)
     def _():
@@ -266,7 +267,6 @@
 
     @pl.when(step == last - 1)
     def _():
-        spread.begin(last)
         spread.third(last - 1)
         spread.fourth(last - 2)
         spread.fifth(last - 3)

time: 110 us -> 109 us (level)
  no operation moved by 1% of the time
where the time goes in v7:
time: 109 us; the launch traced here: 108 us
  Pallas kernels  67.8 us (62%)
  waiting for transfers between devices  13.8 us (13%)
  local copies, waits for them, and re-layouts  13.4 us (12%)
  starting transfers between devices  10.8 us (10%)
  other arithmetic  1.41 us (1%)
    pallas_call x1, Pallas kernels, run_attention(): pl.pallas_call(column_attention, grid=(count_res,), in_specs=[pl.BlockSpe...  43.6 us
    pallas_call x1, Pallas kernels, run_pair(): pl.pallas_call(pair_tile, grid=(4,), in_specs=[FULL, FULL] + [resident(on...  24.2 us
    all_to_all x1, waiting for transfers between devices, shards(): lax.all_to_all(fragments, ('row', 'col'), split_axis=2, concat_axis=0, ti...  13.8 us
    all_to_all x1, starting transfers between devices, shards(): lax.all_to_all(fragments, ('row', 'col'), split_axis=2, concat_axis=0, ti...  10.8 us
    unnamed x18, local copies, waits for them, and re-layouts  7.16 us
    reshape x1, local copies, waits for them, and re-layouts, shards(): alignment_output = updated.reshape(seqs, res_here, width)  2.64 us
  transfers between devices with their start and end apart: 1, of which 1 were waited for; matrix products, arithmetic and copies ran while one was open for 4% of the time, Pallas kernels for 0%

profile of v7, /device:TPU:7, one launch (start us, length us, event | category | flops | bytes accessed | tf_op | source)
XLA Modules:
  0.0 107.8 jit_solution(12585804452808424291)
XLA Ops:
  0.6 0.0 copy-start.2
  0.6 0.0 copy-start.3
  0.7 0.0 copy-start.5
  0.7 0.0 copy-start.1
  0.7 0.0 copy-start
  0.7 0.0 copy-start.4
  0.7 3.0 %copy.27 = bf16[4,512,256]{2,0,1:T(4,128)(2,1)} copy(bf16[4,512,256]{2,1,0:T(8,128)(2,1)} %param.18) | data formatting | bytes 2097152 | tf_op args[0]
  3.7 10.8 %all-to-all-start = ((bf16[1,4,128,4,256]{4,1,3,0,2:T(4,128)(2,1)}), bf16[1,4,128,4,256]{4,1,3,0,2:T(4,128)(2,1)S(1)}, u32[]{:S(2)}, u32[]{:S(2)}) async-start(bf16[1,4,128,4,256]{4,1,3,0,2:T(4,128)(2,1)} %bitcast), calls=%async_computation | async-start | bytes 2097152 | tf_op jit(solution)/shard_map/all_to_all | solution.py:538
  14.5 0.0 copy-done.2
  14.5 0.1 copy.30
  14.6 0.0 copy-done.3
  14.6 0.1 copy.29
  14.8 0.0 copy-done.5
  14.8 0.6 pad.8.feat_ref
  15.4 0.0 copy-done.1
  15.4 0.6 pad.9.offset_ref
  16.0 0.0 copy-done
  16.0 0.8 copy.31
  16.8 0.0 copy-done.4
  16.8 0.1 copy.32
  16.9 0.1 pad.14.clone
  17.0 0.7 pad_maximum_fusion.bins_ref
  17.7 0.7 maximum_maximum_fusion.factor_ref
  18.4 13.8 %all-to-all-done = bf16[1,4,128,4,256]{4,1,3,0,2:T(4,128)(2,1)S(1)} async-done(((bf16[1,4,128,4,256]{4,1,3,0,2:T(4,128)(2,1)}), bf16[1,4,128,4,256]{4,1,3,0,2:T(4,128)(2,1)S(1)}, u32[]{:S(2)}, u32[]{:S(2)}) %all-to-all-start) | async-done | bytes 1048608 | tf_op jit(solution)/shard_map/all_to_all | solution.py:538
  32.2 0.4 copy.28
  32.5 1.1 %reshape.23 = bf16[512,4,256]{2,0,1:T(8,128)(2,1)} reshape(bf16[128,1,4,1,4,256]{5,2,0,4,3,1:T(4,128)(2,1)S(1)} %copy.28) | data formatting | bytes 2097152 | tf_op jit(solution)/shard_map/reshape | solution.py:539
  33.6 43.6 %column_attention.1 = (bf16[512,1024]{1,0:T(8,128)(2,1)}, bf16[16,5,32,512]{3,2,1,0:T(8,128)(2,1)}, bf16[8,5,32,512]{3,2,1,0:T(8,128)(2,1)}) custom-call(bf16[4,512,256]{2,1,0:T(8,128)(2,1)} %bitcast.11, bf16[16,256]{1,0:T(8,128)(2,1)} %pad.8.feat_ref, bf16[256,256]{1,0:T(8,128)(2,1)} %wq_ref.1, bf16[256,256]{1,0:T(8,128)(2,1)} %wk_ref.1, ...), custom_call_target="tpu_custom_call" | custom-call | tf_op jit(solution)/shard_map/column_attention/pallas_call | solution.py:295
  77.3 2.6 %reshape.24 = bf16[512,4,256]{2,1,0:T(4,128)(2,1)} reshape(bf16[512,1024]{1,0:T(8,128)(2,1)} %get-tuple-element.8) | data formatting | bytes 2097152 | tf_op jit(solution)/shard_map/reshape | solution.py:560
  79.9 24.2 %pair_tile.1 = (bf16[64,32,128]{2,1,0:T(8,128)(2,1)}, bf16[64,32,64]{2,1,0:T(8,128)(2,1)}) custom-call(bf16[16,5,32,512]{3,2,1,0:T(8,128)(2,1)} %get-tuple-element.9.a_ref, bf16[8,5,32,512]{3,2,1,0:T(8,128)(2,1)} %get-tuple-element.10.b_ref, bf16[128,128]{1,0:T(8,128)(2,1)} %pad.9.offset_ref, bf16[1024,128]{1,0:T(8,128)(2,1)} %bitcast.13, ...), custom_call_target="tpu_custom_call" | custom-call | tf_op jit(solution)/shard_map/pair_tile/pallas_call | solution.py:478
  104.1 1.9 %copy.36 = bf16[64,32,128]{2,1,0:T(8,128)(2,1)} copy(bf16[64,32,128]{2,1,0:T(8,128)(2,1)} %get-tuple-element.17) | data formatting | bytes 1048576
  105.9 1.9 %copy.37 = bf16[64,32,64]{2,1,0:T(8,128)(2,1)} copy(bf16[64,32,64]{2,1,0:T(8,128)(2,1)} %get-tuple-element.18) | data formatting | bytes 524288
  (1 shorter events, 0.0 us)
Async XLA Ops:
  0.6 13.9 %copy-start.2 = (bf16[256,32]{0,1:T(8,128)(2,1)S(1)}, bf16[256,32]{0,1:T(8,128)(2,1)}, u32[]{:S(2)}) copy-start(bf16[256,32]{0,1:T(8,128)(2,1)} %param.28) | copy-start | bytes 49156
  0.6 14.0 %copy-start.3 = (bf16[256,32]{0,1:T(8,128)(2,1)S(1)}, bf16[256,32]{0,1:T(8,128)(2,1)}, u32[]{:S(2)}) copy-start(bf16[256,32]{0,1:T(8,128)(2,1)} %param.27) | copy-start | bytes 49156
  0.7 14.1 %copy-start.5 = (bf16[4,256]{1,0:T(4,128)(2,1)S(1)}, bf16[4,256]{1,0:T(4,128)(2,1)}, u32[]{:S(2)}) copy-start(bf16[4,256]{1,0:T(4,128)(2,1)} %param.19) | copy-start | bytes 6148
  0.7 14.7 %copy-start.1 = (bf16[65,128]{1,0:T(8,128)(2,1)S(1)}, bf16[65,128]{1,0:T(8,128)(2,1)}, u32[]{:S(2)}) copy-start(bf16[65,128]{1,0:T(8,128)(2,1)} %param.32) | copy-start | bytes 49924
  0.7 15.3 %copy-start = (bf16[1024,128]{1,0:T(8,128)(2,1)S(1)}, bf16[1024,128]{1,0:T(8,128)(2,1)}, u32[]{:S(2)}) copy-start(bf16[1024,128]{1,0:T(8,128)(2,1)} %param.29) | copy-start | bytes 786436
  0.7 16.1 %copy-start.4 = (bf16[128,64]{0,1:T(8,128)(2,1)S(1)}, bf16[128,64]{0,1:T(8,128)(2,1)}, u32[]{:S(2)}) copy-start(bf16[128,64]{0,1:T(8,128)(2,1)} %param.35) | copy-start | bytes 49156
  3.7 28.4 %all-to-all-start = ((bf16[1,4,128,4,256]{4,1,3,0,2:T(4,128)(2,1)}), bf16[1,4,128,4,256]{4,1,3,0,2:T(4,128)(2,1)S(1)}, u32[]{:S(2)}, u32[]{:S(2)}) async-start(bf16[1,4,128,4,256]{4,1,3,0,2:T(4,128)(2,1)} %bitcast), calls=%async_computation | async-start | bytes 2097152 | tf_op jit(solution)/shard_map/all_to_all | solution.py:538
